TPU v7x, 128 devices: a whole 4x4x4 slice. The times are simulated.
128 devices in a mesh: col: 2 (over core), row: 64 (over z, y, x).
Axes of the slice: x: 4, y: 4, z: 4, core: 2. Of those that a mesh axis runs over, the one named last changes fastest.
Arguments:
- img_emb: bfloat16 [32768, 768], P(('row', 'col'))
- txt_emb: bfloat16 [32768, 768], P(('row', 'col'))
- log_scale: float32 [], replicated
Outputs:
- output 1: float32 [], replicated
- output 2: bfloat16 [32768, 768], P(('row', 'col'))
- output 3: bfloat16 [32768, 768], P(('row', 'col'))
- output 4: float32 [], replicated
All inputs are finite; a program needn't handle non-finite values.
Results may differ from a plain program's by a relative error of at most 0.001.
Values are sent between devices in bfloat16 or wider.
A program may use at most 1 GiB of HBM per device.

v0:
```python
import jax
import jax.numpy as jnp
from jax import lax
from jax.sharding import PartitionSpec as P, NamedSharding


def solution(mesh):
    n_row = mesh.shape["row"]
    n_col = mesh.shape["col"]
    batch_spec = P(("row", "col"), None)
    both_axes = ("row", "col")

    def local_tile(img_loc, txt_loc, log_scale):
        rows_dev = img_loc.shape[0]
        batch_size = rows_dev * n_row * n_col
        inv_count = 1.0 / (2 * batch_size)
        row_id = lax.axis_index("row")
        col_id = lax.axis_index("col")
        logit_scale = jnp.exp(log_scale)
        img_block = lax.all_gather(img_loc, "col", tiled=True)
        txt_block = lax.all_gather(txt_loc, "row", tiled=True)
        logits = logit_scale * jnp.einsum("id,jd->ij", img_block, txt_block, preferred_element_type=jnp.float32)
        row_glob = row_id * (rows_dev * n_col) + jnp.arange(rows_dev * n_col)
        col_pos = jnp.arange(rows_dev * n_row)
        col_glob = ((col_pos // rows_dev) * n_col + col_id) * rows_dev + col_pos % rows_dev
        diag_mask = row_glob[:, None] == col_glob[None, :]
        row_max = jnp.max(logits, axis=1)
        row_exp = jnp.exp(logits - row_max[:, None])
        row_part = jnp.sum(row_exp, axis=1)
        col_max = jnp.max(logits, axis=0)
        col_exp = jnp.exp(logits - col_max[None, :])
        col_part = jnp.sum(col_exp, axis=0)
        row_top = lax.pmax(row_max, "col")
        row_tot = lax.psum(row_part * jnp.exp(row_max - row_top), "col")
        row_lse = row_top + jnp.log(row_tot)
        col_top = lax.pmax(col_max, "row")
        col_tot = lax.psum(col_part * jnp.exp(col_max - col_top), "row")
        col_lse = col_top + jnp.log(col_tot)
        own_block = lax.dynamic_slice(logits, (col_id * rows_dev, row_id * rows_dev), (rows_dev, rows_dev))
        own_diag = jnp.diagonal(own_block)
        own_row_lse = lax.dynamic_slice(row_lse, (col_id * rows_dev,), (rows_dev,))
        own_col_lse = lax.dynamic_slice(col_lse, (row_id * rows_dev,), (rows_dev,))
        loss_part = jnp.sum(own_row_lse + own_col_lse - 2.0 * own_diag)
        total_loss = lax.psum(loss_part, both_axes) * inv_count
        row_factor = jnp.exp(row_max - row_lse) * inv_count
        col_factor = jnp.exp(col_max - col_lse) * inv_count
        grad_tile = row_exp * row_factor[:, None] + col_exp * col_factor[None, :] - jnp.where(diag_mask, 2.0 * inv_count, 0.0)
        d_log_scale = lax.psum(jnp.sum(grad_tile * logits), both_axes)
        grad_bf = grad_tile.astype(jnp.bfloat16)
        img_part = jnp.einsum("ij,jd->id", grad_bf, txt_block, preferred_element_type=jnp.float32)
        img_sum = lax.psum_scatter(img_part, "col", scatter_dimension=0, tiled=True)
        d_img = (logit_scale * img_sum).astype(jnp.bfloat16)
        txt_part = jnp.einsum("ij,id->jd", grad_bf, img_block, preferred_element_type=jnp.float32)
        txt_sum = lax.psum_scatter(txt_part, "row", scatter_dimension=0, tiled=True)
        d_txt = (logit_scale * txt_sum).astype(jnp.bfloat16)
        return total_loss, d_img, d_txt, d_log_scale

    return jax.shard_map(local_tile, mesh=mesh, in_specs=(batch_spec, batch_spec, P()), out_specs=(P(), batch_spec, batch_spec, P()), check_vma=False)
```

profile of v0, /device:TPU:1, one launch (start us, length us, event | category | flops | bytes accessed | tf_op | source)
XLA Modules:
  0.0 794.3 jit_solution(6677830852584103210)
XLA Ops:
  7.2 0.0 all-gather.2.cloned.1.call-start
  7.2 0.7 all-gather.2.cloned.1.call-update
  7.9 0.0 all-reduce.4.cloned.1.call-start
  8.6 3.4 all_gather.6
  12.0 132.7 %all-gather.2.cloned.1.call-done = bf16[16384,768]{1,0:T(8,128)(2,1)} async-done(((bf16[256,768]{1,0:T(8,128)(2,1)}), bf16[16384,768]{1,0:T(8,128)(2,1)}) %all-gather.2.cloned.1.call-update) | async-done | bytes 25165840 | tf_op jit(solution)/shard_map/all_gather | solution.py:21
  144.8 26.9 %fusion.14 = (f32[512]{0:T(512)S(1)}, f32[16384]{0:T(1024)}, f32[512,16384]{1,0:T(8,128)}) fusion(bf16[512,768]{1,0:T(8,128)(2,1)S(1)} %all_gather.6, bf16[16384,768]{1,0:T(8,128)(2,1)} %all-gather.2.cloned.1.call-done, f32[]{:T(128)S(6)} %exp.21), kind=kOutput, calls=%fused_computation.35 | convolution fusion | flops 12910051328 | bytes 59574276 | tf_op jit(solution)/shard_map/id,jd->ij/dot_general | solution.py:22
  171.7 0.0 copy-start
  171.7 0.0 all-reduce.4.cloned.1.call-update
  171.7 0.0 all-reduce.6.cloned.1.call-start
  171.7 3.1 pmax.14
  174.8 15.7 %fusion = (f32[512]{0:T(512)S(1)}, f32[16384]{0:T(1024)S(1)}) fusion(f32[512,16384]{1,0:T(8,128)} %get-tuple-element.16, f32[512]{0:T(512)S(1)} %get-tuple-element.6, f32[16384]{0:T(1024)} %get-tuple-element.7), kind=kLoop, calls=%fused_computation.5 | loop fusion | flops 33537536 | bytes 33689600 | tf_op jit(solution)/shard_map/reduce_sum | solution.py:29
  190.5 2.5 psum.28
  193.0 102.9 %all-reduce.4.cloned.1.call-done = f32[16384]{0:T(1024)} async-done(((f32[16384]{0:T(1024)}), f32[16384]{0:T(1024)}) %all-reduce.4.cloned.1.call-update) | async-done | bytes 65552 | tf_op jit(solution)/shard_map/pmax | solution.py:36
  295.8 0.0 copy-done
  295.8 1.5 exponential_multiply_fusion.1
  297.3 0.0 all-reduce.6.cloned.1.call-update
  297.3 0.2 reduce-scatter.3.cloned.1.call-start
  297.6 127.9 %all-reduce.6.cloned.1.call-done = f32[16384]{0:T(1024)} async-done(((f32[16384]{0:T(1024)}), f32[16384]{0:T(1024)}) %all-reduce.6.cloned.1.call-update) | async-done | bytes 65552 | tf_op jit(solution)/shard_map/psum | solution.py:37
  425.4 0.9 exponential_multiply_fusion
  426.3 23.6 %fusion.2 = (bf16[512,16384]{1,0:T(8,128)(2,1)}, f32[]{:T(128)}) fusion(f32[512,16384]{1,0:T(8,128)} %get-tuple-element.16, s32[16384]{0:T(1024)S(1)} %fusion.12, f32[16384]{0:T(1024)S(1)} %get-tuple-element.12, f32[512]{0:T(512)S(1)} %get-tuple-element.10, f32[16384]{0:T(1024)S(1)} %copy-done, f32[512]{0:T(512)S(1)} %get-tuple-element.6, s32[512]{0:T(512)S(1)} %iota_add_fusion), kind=kLoop, calls=%fused_computation.7 | loop fusion | flops 92274688 | bytes 50534404 | tf_op jit(solution)/shard_map/convert_element_type | solution.py:49
  449.9 21.4 %fusion.15 = f32[512,768]{1,0:T(8,128)} fusion(bf16[512,16384]{1,0:T(8,128)(2,1)} %get-tuple-element.14, bf16[16384,768]{1,0:T(8,128)(2,1)} %all-gather.2.cloned.1.call-done), kind=kOutput, calls=%fused_computation.36 | convolution fusion | flops 12884901888 | bytes 43515904 | tf_op jit(solution)/shard_map/ij,jd->id/dot_general | solution.py:50
  471.4 0.0 reduce-scatter.3.cloned.1.call-update
  471.4 0.3 reduce-scatter.5.cloned.1.call-start
  471.6 26.9 %fusion.16 = f32[16384,768]{1,0:T(8,128)} fusion(bf16[512,16384]{1,0:T(8,128)(2,1)} %get-tuple-element.14, bf16[512,768]{1,0:T(8,128)(2,1)S(1)} %all_gather.6), kind=kOutput, calls=%fused_computation.37 | convolution fusion | flops 12884901888 | bytes 67895296 | tf_op jit(solution)/shard_map/ij,id->jd/dot_general | solution.py:53
  498.6 0.0 reduce-scatter.5.cloned.1.call-update
  498.6 1.0 dynamic_slice.11
  499.6 2.3 gather_fusion
  501.9 0.7 subtract_reduce_fusion
  502.6 65.8 %all-reduce = (f32[]{:T(128)}, f32[]{:T(128)}) all-reduce(f32[]{:T(128)} %subtract_reduce_fusion, f32[]{:T(128)} %get-tuple-element.15), channel_id=1, replica_groups=mesh['col'=2,'row'=64] {'row','col'}, use_global_device_ids=true, to_apply=%region_9.10 | all-reduce | flops 2 | bytes 16 | tf_op jit(solution)/shard_map/psum | solution.py:44
  569.0 0.0 reduce-scatter.3.cloned.1.call-done
  569.1 1.9 multiply_convert_fusion.1
  571.0 213.7 %reduce-scatter.5.cloned.1.call-done = f32[256,768]{1,0:T(8,128)} async-done(((f32[16384,768]{1,0:T(8,128)}), f32[256,768]{1,0:T(8,128)}) %reduce-scatter.5.cloned.1.call-update) | async-done | bytes 786448 | tf_op jit(solution)/shard_map/reduce_scatter | solution.py:54
  784.7 1.9 multiply_convert_fusion
  (5 shorter events, 0.1 us)
Async XLA Ops:
  7.2 137.6 %all-gather.2.cloned.1.call-start = ((), (), s32[]{:S(2)}) async-start(), calls=%async_computation.2 | async-start | bytes 25559040 | tf_op jit(solution)/shard_map/all_gather | solution.py:21
  7.9 287.9 %all-reduce.4.cloned.1.call-start = ((), (), s32[]{:S(2)}) async-start(), calls=%async_computation.3 | async-start | bytes 131072 | tf_op jit(solution)/shard_map/pmax | solution.py:36
  171.7 124.2 %copy-start = (f32[16384]{0:T(1024)S(1)}, f32[16384]{0:T(1024)}, u32[]{:S(2)}) copy-start(f32[16384]{0:T(1024)} %get-tuple-element.7) | copy-start | bytes 196612
  171.7 253.8 %all-reduce.6.cloned.1.call-start = ((), (), s32[]{:S(2)}) async-start(), calls=%async_computation.4 | async-start | bytes 131072 | tf_op jit(solution)/shard_map/psum | solution.py:37
  297.3 271.7 %reduce-scatter.3.cloned.1.call-start = ((), (), s32[]{:S(2)}) async-start(), calls=%async_computation.5 | async-start | bytes 2359296 | tf_op jit(solution)/shard_map/reduce_scatter | solution.py:51
  471.4 313.3 %reduce-scatter.5.cloned.1.call-start = ((), (), s32[]{:S(2)}) async-start(), calls=%async_computation.6 | async-start | bytes 51118080 | tf_op jit(solution)/shard_map/reduce_scatter | solution.py:54
Sparse Core Ops, SparseCore 0:
  10.7 133.9 all-gather.1
  171.8 123.9 all-reduce.3
  301.1 124.3 all-reduce.5
  471.5 12.2 reduce-scatter.2
  498.7 285.9 reduce-scatter.4
where the time goes:
time: 796 us; the launch traced here: 794 us
  waiting for transfers between devices  578 us (73%)
  matrix products  75.2 us (9%)
  blocking collectives  74.7 us (9%)
  other arithmetic  46.2 us (6%)
  between operations  16.3 us (2%)
    reduce_scatter x1, waiting for transfers between devices, local_tile(): txt_sum = lax.psum_scatter(txt_part, 'row', scatter_dimension=0, tiled=True)  214 us
    all_gather x1, waiting for transfers between devices, local_tile(): txt_block = lax.all_gather(txt_loc, 'row', tiled=True)  133 us
    psum x1, waiting for transfers between devices, local_tile(): col_tot = lax.psum(col_part * jnp.exp(col_max - col_top), 'row')  128 us
    pmax x1, waiting for transfers between devices, local_tile(): col_top = lax.pmax(col_max, 'row')  103 us
    psum x1, blocking collectives, local_tile(): total_loss = lax.psum(loss_part, both_axes) * inv_count  65.8 us
    dot_general x1, matrix products, local_tile(): jnp.einsum('ij,id->jd', grad_bf, img_block, preferred_element_type=jnp.fl...  26.9 us
    dot_general x1, matrix products, local_tile(): jnp.einsum('id,jd->ij', img_block, txt_block, preferred_element_type=jnp....  26.9 us
    convert_element_type x1, other arithmetic, local_tile(): grad_bf = grad_tile.astype(jnp.bfloat16)  23.6 us
  transfers between devices with their start and end apart: 5, of which 4 were waited for; matrix products, arithmetic and copies ran while one was open for 6% of the time, Pallas kernels for 0%

commit v1 on v0

v1 whole, which is shorter than its diff:
```python
import functools

import jax
import jax.numpy as jnp
from jax import lax
from jax.experimental import pallas as pl
from jax.experimental.pallas import tpu as pltpu
from jax.sharding import PartitionSpec as P

MESH = pl.DeviceIdType.MESH
F32 = jnp.float32
BF16 = jnp.bfloat16
VMEM_LIMIT = 64_000_000


class Grid:
    def __init__(self):
        row = lax.axis_index("row")
        self.c = lax.axis_index("col")
        self.z = row // 16
        self.y = (row // 4) % 4
        self.x = row % 4

    def dev(self, z, y, x, c):
        return {"row": (z * 4 + y) * 4 + x, "col": c}

    def y_a(self):
        return self.y + 1 - 2 * (self.y % 2)

    def y_b(self):
        return 3 - self.y

    def img_peer(self, dy, dz):
        y = self.y_a() if dy else self.y
        return self.dev((self.z + dz) % 4, y, self.x, self.c)

    def txt_peer(self, dc, dy, dx):
        y = self.y_b() if dy else self.y
        c = 1 - self.c if dc else self.c
        return self.dev(self.z, y, (self.x + dx) % 4, c)


class Net:
    def __init__(self, send_sems, recv_sems):
        self.send_sems, self.recv_sems, self.copies = send_sems, recv_sems, []

    def send(self, src, dst, peer):
        i = len(self.copies)
        copy = pltpu.make_async_remote_copy(
            src_ref=src, dst_ref=dst, send_sem=self.send_sems.at[i], recv_sem=self.recv_sems.at[i],
            device_id=peer, device_id_type=MESH)
        copy.start()
        self.copies.append(copy)
        return copy

    def finish(self):
        for copy in self.copies:
            copy.wait_send()


def greet(peers):
    barrier = pltpu.get_barrier_semaphore()
    for peer in peers:
        pl.semaphore_signal(barrier, inc=1, device_id=peer, device_id_type=MESH)
    pl.semaphore_wait(barrier, len(peers))


def neighbours(g):
    return [g.img_peer(0, 1), g.img_peer(0, 3), g.img_peer(1, 0), g.txt_peer(0, 0, 1), g.txt_peer(0, 0, 3),
            g.txt_peer(0, 1, 0), g.txt_peer(1, 0, 0)]


N_GATHER = 9 + 9 + 10


def gather_kernel(n, img_ref, txt_ref, img_all, txt_all, local_sems, send_sems, recv_sems):
    g = Grid()
    own = [pltpu.make_async_copy(img_ref, img_all.at[pl.ds(0, n)], local_sems.at[0]),
           pltpu.make_async_copy(txt_ref, txt_all.at[pl.ds(0, n)], local_sems.at[1])]
    for copy in own:
        copy.start()
    greet(neighbours(g))
    net = Net(send_sems, recv_sems)
    h = n // 2

    def slot(ref, k, lo=0, size=n):
        return ref.at[pl.ds(k * n + lo, size)]

    def ring(ref, peer_plus, peer_minus, peer_y):
        return dict(ref=ref, plus=peer_plus, minus=peer_minus, y=peer_y)

    img = ring(img_all, g.img_peer(0, 1), g.img_peer(0, 3), g.img_peer(1, 0))
    txt = ring(txt_all, g.txt_peer(0, 0, 1), g.txt_peer(0, 0, 3), g.txt_peer(0, 1, 0))
    core = g.txt_peer(1, 0, 0)
    for r, src in ((img, img_ref), (txt, txt_ref)):
        r["y0"] = net.send(src, slot(r["ref"], 4), r["y"])
        r["p0"] = net.send(src, slot(r["ref"], 3), r["plus"])
        r["m0"] = net.send(src, slot(r["ref"], 1), r["minus"])
    cross = [net.send(txt_ref, slot(txt_all, 8), core)]
    for r in (img, txt):
        r["y0"].wait_recv()
        r["p1"] = net.send(slot(r["ref"], 4), slot(r["ref"], 7), r["plus"])
        r["m1"] = net.send(slot(r["ref"], 4), slot(r["ref"], 5), r["minus"])
    cross.append(net.send(slot(txt_all, 4), slot(txt_all, 12), core))
    for dy in (0, 1):
        for r in (img, txt):
            ref, b = r["ref"], 4 * dy
            r["p%d" % dy].wait_recv()
            r["fp%d" % dy] = net.send(slot(ref, b + 3, 0, h), slot(ref, b + 2, 0, h), r["plus"])
            r["m%d" % dy].wait_recv()
            r["fm%d" % dy] = net.send(slot(ref, b + 1, h, h), slot(ref, b + 2, h, h), r["minus"])
        cross.append(net.send(slot(txt_all, 4 * dy + 3), slot(txt_all, 8 + 4 * dy + 3), core))
        cross.append(net.send(slot(txt_all, 4 * dy + 1), slot(txt_all, 8 + 4 * dy + 1), core))
    for dy in (0, 1):
        for r in (txt, img):
            r["fp%d" % dy].wait_recv()
            if r is txt:
                cross.append(net.send(slot(txt_all, 4 * dy + 2, 0, h), slot(txt_all, 8 + 4 * dy + 2, 0, h), core))
            r["fm%d" % dy].wait_recv()
            if r is txt:
                cross.append(net.send(slot(txt_all, 4 * dy + 2, h, h), slot(txt_all, 8 + 4 * dy + 2, h, h), core))
    for copy in cross:
        copy.wait_recv()
    for copy in own:
        copy.wait()
    net.finish()


def gather(img, txt):
    n, d = img.shape
    return pl.pallas_call(
        functools.partial(gather_kernel, n),
        out_shape=[jax.ShapeDtypeStruct((8 * n, d), BF16), jax.ShapeDtypeStruct((16 * n, d), BF16)],
        in_specs=[pl.BlockSpec(memory_space=pltpu.VMEM)] * 2,
        out_specs=[pl.BlockSpec(memory_space=pl.ANY)] * 2,
        scratch_shapes=[pltpu.SemaphoreType.DMA((2,)), pltpu.SemaphoreType.DMA((N_GATHER,)),
                        pltpu.SemaphoreType.DMA((N_GATHER,))],
        compiler_params=pltpu.CompilerParams(collective_id=0, has_side_effects=True, vmem_limit_bytes=VMEM_LIMIT),
        name="gather_blocks")(img, txt)


BN = 512
CM = 256


def pass1_kernel(scale_ref, img_ref, txt_ref, e_ref, rs_ref, rl_ref, cs_ref, cl_ref):
    j = pl.program_id(0)
    scale = scale_ref[0]
    rows = img_ref.shape[0]

    @pl.when(j == 0)
    def _():
        rs_ref[...] = jnp.zeros_like(rs_ref)
        rl_ref[...] = jnp.zeros_like(rl_ref)

    cs_ref[...] = jnp.zeros_like(cs_ref)
    cl_ref[...] = jnp.zeros_like(cl_ref)

    def step(i, carry):
        at = pl.ds(pl.multiple_of(i * CM, CM), CM)
        dots = lax.dot_general(img_ref[at, :], txt_ref[...], (((1,), (1,)), ((), ())), preferred_element_type=F32)
        logits = scale * dots
        e = jnp.exp(logits)
        el = e * logits
        e_ref[at, :] = e
        rs, rl = rs_ref[at, :], rl_ref[at, :]
        for q in range(BN // 128):
            lanes = slice(q * 128, (q + 1) * 128)
            rs += e[:, lanes]
            rl += el[:, lanes]
        rs_ref[at, :] = rs
        rl_ref[at, :] = rl
        cs_ref[...] += jnp.sum(e.reshape(CM // 8, 8, BN), axis=0)
        cl_ref[...] += jnp.sum(el.reshape(CM // 8, 8, BN), axis=0)
        return carry

    lax.fori_loop(0, rows // CM, step, 0)


def pass1(scale, img_all, txt_all):
    m, d = img_all.shape
    n = txt_all.shape[0]
    whole = lambda j: (0, 0)
    return pl.pallas_call(
        pass1_kernel,
        grid=(n // BN,),
        out_shape=[jax.ShapeDtypeStruct((m, n), F32), jax.ShapeDtypeStruct((m, 128), F32),
                   jax.ShapeDtypeStruct((m, 128), F32), jax.ShapeDtypeStruct((8, n), F32),
                   jax.ShapeDtypeStruct((8, n), F32)],
        in_specs=[pl.BlockSpec(memory_space=pltpu.SMEM), pl.BlockSpec((m, d), whole),
                  pl.BlockSpec((BN, d), lambda j: (j, 0))],
        out_specs=[pl.BlockSpec((m, BN), lambda j: (0, j)), pl.BlockSpec((m, 128), whole),
                   pl.BlockSpec((m, 128), whole), pl.BlockSpec((8, BN), lambda j: (0, j)),
                   pl.BlockSpec((8, BN), lambda j: (0, j))],
        compiler_params=pltpu.CompilerParams(dimension_semantics=("arbitrary",), vmem_limit_bytes=VMEM_LIMIT),
        cost_estimate=pl.CostEstimate(flops=2 * m * n * d, bytes_accessed=4 * m * n, transcendentals=m * n),
        name="logits_pass")(scale, img_all, txt_all)


N_SUMS = 7 + 15


def sums_kernel(inv, rs_ref, rl_ref, cs_ref, cl_ref, pos_ref, a_ref, b_ref, part_ref, rbuf, cbuf, send_sems, recv_sems):
    g = Grid()
    img_offs = [(dy, dz) for dy in (0, 1) for dz in range(4) if (dy, dz) != (0, 0)]
    txt_offs = [(dc, dy, dx) for dc in (0, 1) for dy in (0, 1) for dx in range(4) if (dc, dy, dx) != (0, 0, 0)]
    greet([g.img_peer(*o) for o in img_offs] + [g.txt_peer(*o) for o in txt_offs])
    net = Net(send_sems, recv_sems)
    for dc, dy, dx in txt_offs:
        net.send(cs_ref, cbuf.at[dc * 8 + dy * 4 + (4 - dx) % 4], g.txt_peer(dc, dy, dx))
    for dy, dz in img_offs:
        net.send(rs_ref, rbuf.at[dy * 4 + (4 - dz) % 4], g.img_peer(dy, dz))
    for copy in net.copies:
        copy.wait_recv()
    a, b, rtot, ctot = [], [], [], []
    for dy, dz in [(0, 0)] + img_offs:
        k = 2 * (dy * 4 + dz)
        tot = rs_ref[k:k + 2, :]
        for oy, oz in img_offs:
            q = 2 * ((dy ^ oy) * 4 + (dz - oz) % 4)
            tot += rbuf[oy * 4 + oz, q:q + 2, :]
        rtot.append(tot)
        a.append(inv / tot)
        a_ref[k:k + 2, :] = a[-1]
    for dc, dy, dx in [(0, 0, 0)] + txt_offs:
        k = 2 * (dc * 8 + dy * 4 + dx)
        tot = cs_ref[k:k + 2, :]
        for oc, oy, ox in txt_offs:
            q = 2 * ((dc ^ oc) * 8 + (dy ^ oy) * 4 + (dx - ox) % 4)
            tot += cbuf[oc * 8 + oy * 4 + ox, q:q + 2, :]
        ctot.append(tot)
        b.append(inv / tot)
        b_ref[k:k + 2, :] = b[-1]
    pos = pos_ref[...]
    loss = jnp.log(rtot[0]) + jnp.log(ctot[0]) - 2.0 * pos
    dt = -2.0 * pos
    for k in range(8):
        dt += a[k] * (1.0 / inv) * rl_ref[2 * k:2 * k + 2, :]
    for k in range(16):
        dt += b[k] * (1.0 / inv) * cl_ref[2 * k:2 * k + 2, :]
    loss = jnp.sum(loss, axis=0, keepdims=True) * inv
    dt = jnp.sum(dt, axis=0, keepdims=True) * inv
    part_ref[...] = jnp.zeros_like(part_ref)
    part_ref[0:1, :] = loss
    part_ref[1:2, :] = dt
    net.finish()


def exchange_sums(inv, rs, rl, cs, cl, pos):
    vmem = pl.BlockSpec(memory_space=pltpu.VMEM)
    return pl.pallas_call(
        functools.partial(sums_kernel, inv),
        out_shape=[jax.ShapeDtypeStruct(rs.shape, F32), jax.ShapeDtypeStruct(cs.shape, F32),
                   jax.ShapeDtypeStruct((8, 128), F32)],
        in_specs=[vmem] * 5,
        out_specs=[vmem] * 3,
        scratch_shapes=[pltpu.VMEM((8,) + rs.shape, F32), pltpu.VMEM((16,) + cs.shape, F32),
                        pltpu.SemaphoreType.DMA((N_SUMS,)), pltpu.SemaphoreType.DMA((N_SUMS,))],
        compiler_params=pltpu.CompilerParams(collective_id=1, has_side_effects=True),
        name="exchange_sums")(rs, rl, cs, cl, pos)


CI = 512


def pass2_kernel(inv, n, img_ref, txt_ref, e_ref, a_ref, b_ref, dimg_ref, dtxt_ref, gb_ref, imgt_ref):
    j = pl.program_id(0)
    rows, d = img_ref.shape

    @pl.when(j == 0)
    def _():
        for i in range(rows // 256):
            imgt_ref[:, i * 256:(i + 1) * 256] = img_ref[i * 256:(i + 1) * 256, :].T

    b = b_ref[...]

    def grad_step(i, carry):
        at = pl.ds(pl.multiple_of(i * CM, CM), CM)
        a = a_ref[at, :]
        for q in range(BN // 128):
            lanes = slice(q * 128, (q + 1) * 128)
            gb_ref[at, lanes] = (e_ref[at, lanes] * (a + b[:, lanes])).astype(BF16)
        return carry

    lax.fori_loop(0, rows // CM, grad_step, 0)

    @pl.when(j == 0)
    def _():
        diag = lax.broadcasted_iota(jnp.int32, (n, n), 0) == lax.broadcasted_iota(jnp.int32, (n, n), 1)
        for q in range(n // 128):
            lanes = slice(q * 128, (q + 1) * 128)
            grad = e_ref[0:n, lanes] * (a_ref[0:n, :] + b[:, lanes])
            gb_ref[0:n, lanes] = (grad - jnp.where(diag[:, lanes], 2.0 * inv, 0.0)).astype(BF16)

    def txt_step(i, carry):
        at = pl.ds(pl.multiple_of(i * 256, 256), 256)
        part = jnp.dot(imgt_ref[at, :], gb_ref[...], preferred_element_type=F32)
        for q in range(BN // n):
            dtxt_ref[q, at, :] = part[:, q * n:(q + 1) * n]
        return carry

    lax.fori_loop(0, d // 256, txt_step, 0)

    def img_step(first, i, carry):
        at = pl.ds(pl.multiple_of(i * CI, CI), CI)
        part = jnp.dot(gb_ref[at, :], txt_ref[...], preferred_element_type=F32)
        dimg_ref[at, :] = part if first else dimg_ref[at, :] + part
        return carry

    @pl.when(j == 0)
    def _():
        lax.fori_loop(0, rows // CI, functools.partial(img_step, True), 0)

    @pl.when(j > 0)
    def _():
        lax.fori_loop(0, rows // CI, functools.partial(img_step, False), 0)


def pass2(inv, n, img_all, txt_all, e, a, b):
    m, d = img_all.shape
    nt = txt_all.shape[0]
    whole = lambda j: (0, 0)
    return pl.pallas_call(
        functools.partial(pass2_kernel, inv, n),
        grid=(nt // BN,),
        out_shape=[jax.ShapeDtypeStruct((m, d), F32), jax.ShapeDtypeStruct((nt // n, d, n), F32)],
        in_specs=[pl.BlockSpec((m, d), whole), pl.BlockSpec((BN, d), lambda j: (j, 0)),
                  pl.BlockSpec((m, BN), lambda j: (0, j)), pl.BlockSpec((m, 128), whole),
                  pl.BlockSpec((1, BN), lambda j: (0, j))],
        out_specs=[pl.BlockSpec((m, d), whole), pl.BlockSpec((BN // n, d, n), lambda j: (j, 0, 0))],
        scratch_shapes=[pltpu.VMEM((m, BN), BF16), pltpu.VMEM((d, m), BF16)],
        compiler_params=pltpu.CompilerParams(dimension_semantics=("arbitrary",), vmem_limit_bytes=VMEM_LIMIT),
        cost_estimate=pl.CostEstimate(flops=4 * m * nt * d, bytes_accessed=4 * m * nt, transcendentals=0),
        name="grad_pass")(img_all, txt_all, e, a, b)


N_REDUCE = 8 + 2 * (4 + 18 + 1) + 22


class Ring:
    def __init__(self, net, acc, buf, ybuf, rows, cut, plus, minus, pair):
        self.net, self.acc, self.buf, self.ybuf = net, acc, buf, ybuf
        self.cut, self.rows = cut, rows
        self.plus, self.minus, self.pair = plus, minus, pair
        self.streams = {}

    def pair_first(self):
        lo, size = self.cut, self.rows - self.cut
        self.early = {d: self.net.send(self.acc.at[4 + d, pl.ds(lo, size)], self.ybuf.at[d, pl.ds(lo, size)], self.pair)
                      for d in (2, 1, 3, 0)}

    def pair_add(self):
        lo, size = self.cut, self.rows - self.cut
        for d in (2, 1, 3, 0):
            self.early[d].wait_recv()
            self.acc[d, lo:lo + size] += self.ybuf[d, lo:lo + size]

    def start(self, name, dy, lo, size):
        h, b = size // 2, 4 * dy
        acc, buf, send = self.acc, self.buf, self.net.send
        s = dict(lo=lo, h=h, b=b)
        h0, h1 = pl.ds(lo, h), pl.ds(lo + h, h)
        s["a_plus"] = send(acc.at[b + 2, h0], buf.at[b + 2, h0], self.plus)
        s["a_minus"] = send(acc.at[b + 2, h1], buf.at[b + 2, h1], self.minus)
        s["b_plus_h1"] = send(acc.at[b + 1, h1], buf.at[b + 3, h1], self.plus)
        s["b_minus_h0"] = send(acc.at[b + 3, h0], buf.at[b + 1, h0], self.minus)
        self.streams[name] = s

    def middle(self, name):
        s = self.streams[name]
        acc, buf, send = self.acc, self.buf, self.net.send
        lo, h, b = s["lo"], s["h"], s["b"]
        h0, h1 = pl.ds(lo, h), pl.ds(lo + h, h)
        s["a_plus"].wait_recv()
        acc[b + 1, lo:lo + h] += buf[b + 2, lo:lo + h]
        s["b_plus_h0"] = send(acc.at[b + 1, h0], buf.at[b + 3, h0], self.plus)
        s["a_minus"].wait_recv()
        acc[b + 3, lo + h:lo + 2 * h] += buf[b + 2, lo + h:lo + 2 * h]
        s["b_minus_h1"] = send(acc.at[b + 3, h1], buf.at[b + 1, h1], self.minus)

    def end(self, name):
        s = self.streams[name]
        lo, h, b = s["lo"], s["h"], s["b"]
        for key in ("b_plus_h1", "b_minus_h0", "b_plus_h0", "b_minus_h1"):
            s[key].wait_recv()
        self.acc[b, lo:lo + 2 * h] += self.buf[b + 1, lo:lo + 2 * h] + self.buf[b + 3, lo:lo + 2 * h]

    def pair_last(self):
        at = pl.ds(0, self.cut)
        self.late = self.net.send(self.acc.at[4, at], self.buf.at[0, at], self.pair)

    def pair_end(self):
        self.late.wait_recv()
        self.acc[0, 0:self.cut] += self.buf[0, 0:self.cut]


def reduce_kernel(dimg_ref, dtxt_ref, part_ref, img_out, txt_out, part_out, iacc, tacc, ibuf, tbuf, iy, ty, dbuf, pa, pb,
                  psum, local_sems, send_sems, recv_sems):
    g = Grid()
    img_offs = [(dy, dz) for dy in (0, 1) for dz in range(4) if (dy, dz) != (0, 0)]
    txt_offs = [(dc, dy, dx) for dc in (0, 1) for dy in (0, 1) for dx in range(4) if (dc, dy, dx) != (0, 0, 0)]
    loads = {}
    for k in (6, 2, 5, 1, 7, 3, 4, 0):
        loads["t", k] = pltpu.make_async_copy(dtxt_ref.at[k], tacc.at[k], local_sems.at[k])
        loads["i", k] = pltpu.make_async_copy(dimg_ref.at[k], iacc.at[k], local_sems.at[8 + k])
        loads["t", k].start()
        loads["i", k].start()
    greet([g.img_peer(*o) for o in img_offs] + [g.txt_peer(*o) for o in txt_offs])
    net = Net(send_sems, recv_sems)
    core = g.txt_peer(1, 0, 0)
    cross = {k: net.send(dtxt_ref.at[8 + k], dbuf.at[k], core) for k in (6, 5, 7, 4, 2, 1, 3, 0)}
    ia = g.z * 2 + g.y % 2
    ib = (g.x * 2 + g.y // 2) * 2 + g.c
    scal_a = [net.send(part_ref, pa.at[ia], g.img_peer(*o)) for o in img_offs]
    pa[ia] = part_ref[...]

    img = Ring(net, iacc, ibuf, iy, iacc.shape[1], ICUT, g.img_peer(0, 1), g.img_peer(0, 3), g.img_peer(1, 0))
    txt = Ring(net, tacc, tbuf, ty, tacc.shape[1], TCUT, g.txt_peer(0, 0, 1), g.txt_peer(0, 0, 3), g.txt_peer(0, 1, 0))
    for k in (6, 5, 7, 4):
        loads["i", k].wait()
    img.pair_first()
    img.start("1", 1, 0, img.cut)
    for k in (2, 1, 3, 0):
        loads["i", k].wait()
    img.start("0", 0, 0, img.cut)
    for k in (6, 5, 7, 4):
        loads["t", k].wait()
        cross[k].wait_recv()
        tacc[k] += dbuf[k]
    txt.pair_first()
    txt.start("1", 1, 0, txt.cut)
    for k in (2, 1, 3, 0):
        loads["t", k].wait()
        cross[k].wait_recv()
        tacc[k] += dbuf[k]
    txt.start("0", 0, 0, txt.cut)
    for copy in scal_a:
        copy.wait_recv()
    total = pa[0]
    for k in range(1, 8):
        total += pa[k]
    psum[...] = total
    scal_b = [net.send(psum, pb.at[ib], g.txt_peer(*o)) for o in txt_offs]
    pb[ib] = total
    for r in (img, txt):
        r.middle("1")
    for r in (img, txt):
        r.end("1")
        r.pair_last()
        r.middle("0")
    for r in (img, txt):
        r.pair_add()
        r.start("2", 0, r.cut, r.rows - r.cut)
    for copy in scal_b:
        copy.wait_recv()
    total = pb[0]
    for k in range(1, 16):
        total += pb[k]
    part_out[...] = total
    for r in (img, txt):
        r.end("0")
    for r in (img, txt):
        r.middle("2")
    for r in (img, txt):
        r.pair_end()
    for r in (img, txt):
        r.end("2")
    img_out[...] = iacc[0]
    txt_out[...] = tacc[0]
    net.finish()


ICUT = 144
TCUT = 432


def reduce_scatter(dimg, dtxt, part):
    _, n, d = dimg.shape
    vmem = pl.BlockSpec(memory_space=pltpu.VMEM)
    hbm = pl.BlockSpec(memory_space=pl.ANY)
    return pl.pallas_call(
        reduce_kernel,
        out_shape=[jax.ShapeDtypeStruct((n, d), F32), jax.ShapeDtypeStruct((d, n), F32),
                   jax.ShapeDtypeStruct((8, 128), F32)],
        in_specs=[hbm, hbm, vmem],
        out_specs=[vmem] * 3,
        scratch_shapes=[pltpu.VMEM((8, n, d), F32), pltpu.VMEM((8, d, n), F32), pltpu.VMEM((8, n, d), F32),
                        pltpu.VMEM((8, d, n), F32), pltpu.VMEM((4, n, d), F32), pltpu.VMEM((4, d, n), F32),
                        pltpu.VMEM((8, d, n), F32), pltpu.VMEM((8, 8, 128), F32), pltpu.VMEM((16, 8, 128), F32),
                        pltpu.VMEM((8, 128), F32), pltpu.SemaphoreType.DMA((16,)),
                        pltpu.SemaphoreType.DMA((N_REDUCE,)), pltpu.SemaphoreType.DMA((N_REDUCE,))],
        compiler_params=pltpu.CompilerParams(collective_id=2, has_side_effects=True, vmem_limit_bytes=VMEM_LIMIT),
        name="reduce_blocks")(dimg, dtxt, part)


def solution(mesh):
    batch_spec = P(("row", "col"), None)
    shards = mesh.shape["row"] * mesh.shape["col"]

    def local_tile(img_loc, txt_loc, log_scale):
        n, d = img_loc.shape
        inv = 1.0 / (2 * n * shards)
        scale = jnp.exp(log_scale)
        pos = scale * jnp.sum(img_loc.astype(F32) * txt_loc.astype(F32), axis=1)
        img_all, txt_all = gather(img_loc, txt_loc)
        e, rs, rl, cs, cl = pass1(scale.reshape(1), img_all, txt_all)
        rows = lambda v: jnp.sum(v, axis=1).reshape(-1, 128)
        cols = lambda v: jnp.sum(v, axis=0).reshape(-1, 128)
        a, b, part = exchange_sums(inv, rows(rs), rows(rl), cols(cs), cols(cl), pos.reshape(-1, 128))
        a_rows = jnp.broadcast_to(a.reshape(-1, 1), (8 * n, 128))
        dimg, dtxt = pass2(inv, n, img_all, txt_all, e, a_rows, b.reshape(1, -1))
        img_sum, txt_sum, tot = reduce_scatter(dimg.reshape(8, n, d), dtxt, part)
        d_img = (scale * img_sum).astype(BF16)
        d_txt = (scale * txt_sum).T.astype(BF16)
        tot = jnp.sum(tot[0:2], axis=1)
        return tot[0], d_img, d_txt, tot[1]

    return jax.shard_map(local_tile, mesh=mesh, in_specs=(batch_spec, batch_spec, P()),
                         out_specs=(P(), batch_spec, batch_spec, P()), check_vma=False)
```

time: 796 us -> 212 us (0.27)
  waiting for transfers between devices: 578 us -> 0 us
  Pallas kernels: 0 us -> 193 us
  matrix products: 75.2 us -> 0 us
  blocking collectives: 74.7 us -> 0 us
  other arithmetic: 46.2 us -> 13.2 us
  between operations: 16.3 us -> 1.35 us
    reduce_scatter x2 -> x0, waiting for transfers between devices: 214 us -> none  [the longest x1 214 us: local_tile(): txt_sum = lax.psum_scatter(txt_part, 'row', scatter_dimension=0, tiled=True)]
    pallas_call x0 -> x5, Pallas kernels: none -> 193 us  [the longest x1 56.5 us: reduce_scatter(): pl.pallas_call(reduce_kernel, out_shape=[jax.ShapeDtypeStruct((n, d), F32...]
    all_gather x1 -> x0, waiting for transfers between devices: 133 us -> none  [local_tile(): txt_block = lax.all_gather(txt_loc, 'row', tiled=True)]
    psum x1 -> x0, waiting for transfers between devices: 128 us -> none  [local_tile(): col_tot = lax.psum(col_part * jnp.exp(col_max - col_top), 'row')]
    pmax x1 -> x0, waiting for transfers between devices: 103 us -> none  [local_tile(): col_top = lax.pmax(col_max, 'row')]
    dot_general x3 -> x0, matrix products: 75.2 us -> none  [the longest x1 26.9 us: local_tile(): jnp.einsum('ij,id->jd', grad_bf, img_block, preferred_element_type=jnp.fl...]
    psum x2 -> x0, blocking collectives: 68.3 us -> none  [the longest x1 65.8 us: local_tile(): total_loss = lax.psum(loss_part, both_axes) * inv_count]
    convert_element_type x3 -> x2, other arithmetic: 27.5 us -> 3.12 us  [the longest x1 1.92 us: local_tile(): d_img = (scale * img_sum).astype(BF16)]
  transfers between devices with their start and end apart: 5 -> 0, of which waited for: 4 -> 0; matrix products, arithmetic and copies ran while one was open for 6% -> 0% of each run, Pallas kernels for 0% -> 0%
where the time goes in v1:
time: 212 us; the launch traced here: 211 us
  Pallas kernels  193 us (91%)
  other arithmetic  13.2 us (6%)
  local copies, waits for them, and re-layouts  3.5 us (2%)
    pallas_call x1, Pallas kernels, reduce_scatter(): pl.pallas_call(reduce_kernel, out_shape=[jax.ShapeDtypeStruct((n, d), F32...  56.5 us
    pallas_call x1, Pallas kernels, pass2(): pl.pallas_call(functools.partial(pass2_kernel, inv, n), grid=(nt // BN,),...  49.4 us
    pallas_call x1, Pallas kernels, gather(): pl.pallas_call(functools.partial(gather_kernel, n), out_shape=[jax.ShapeD...  39.8 us
    pallas_call x1, Pallas kernels, pass1(): pl.pallas_call(pass1_kernel, grid=(n // BN,), out_shape=[jax.ShapeDtypeSt...  36.4 us
    pallas_call x1, Pallas kernels, exchange_sums(): pl.pallas_call(functools.partial(sums_kernel, inv), out_shape=[jax.ShapeD...  10.8 us
    reduce_sum x2, other arithmetic, local_tile(): rows = lambda v: jnp.sum(v, axis=1).reshape(-1, 128)  4.32 us

profile of v1, /device:TPU:1, one launch (start us, length us, event | category | flops | bytes accessed | tf_op | source)
XLA Modules:
  0.0 211.0 jit_solution(16292487549460823186)
XLA Ops:
  1.3 1.3 multiply_reduce_fusion
  2.6 0.6 multiply_bitcast_fusion.pos_ref
  3.2 39.8 %gather_blocks.1 = (bf16[2048,768]{1,0:T(8,128)(2,1)}, bf16[4096,768]{1,0:T(8,128)(2,1)}) custom-call(bf16[256,768]{1,0:T(8,128)(2,1)} %img_ref.1, bf16[256,768]{1,0:T(8,128)(2,1)} %txt_ref.1), custom_call_target="tpu_custom_call" | custom-call | tf_op jit(solution)/shard_map/gather_blocks/pallas_call | solution.py:131
  43.0 36.4 %logits_pass.1 = (f32[2048,4096]{1,0:T(8,128)}, f32[2048,128]{1,0:T(8,128)}, f32[2048,128]{1,0:T(8,128)}, f32[8,4096]{1,0:T(8,128)}, f32[8,4096]{1,0:T(8,128)}) custom-call(f32[1]{0:T(128)} %bitcast.scale_ref, bf16[2048,768]{1,0:T(8,128)(2,1)} %get-tuple-element.19.img_ref, bf16[4096,768]{1,0:T(8,128)(2,1)} %get-tuple-element.20.txt_ref), custom_call_target="tpu_custom_call" | custom-call | flops 12884901888 | bytes 33554432 | tf_op jit(solution)/shard_map/logits_pass/pallas_call | solution.py:184
  79.4 2.2 %reduce_sum.54 = f32[2048]{0:T(1024)} reduce(f32[2048,128]{1,0:T(8,128)} %get-tuple-element.22, f32[]{:T(128)} %constant.0.clone.1), dimensions={1}, to_apply=%region_0.0 | reduce | flops 260096 | bytes 1056772 | tf_op jit(solution)/shard_map/reduce_sum | solution.py:507
  81.6 2.2 %reduce_sum.55 = f32[2048]{0:T(1024)} reduce(f32[2048,128]{1,0:T(8,128)} %get-tuple-element.23, f32[]{:T(128)} %constant.0.clone.1), dimensions={1}, to_apply=%region_1.0 | reduce | flops 260096 | bytes 1056772 | tf_op jit(solution)/shard_map/reduce_sum | solution.py:507
  83.7 1.5 reduce_sum.56
  85.3 1.5 reduce_sum.57
  86.8 10.8 %exchange_sums.1 = (f32[16,128]{1,0:T(8,128)}, f32[32,128]{1,0:T(8,128)}, f32[8,128]{1,0:T(8,128)}) custom-call(f32[16,128]{1,0:T(8,128)} %bitcast.17, f32[16,128]{1,0:T(8,128)} %bitcast.18, f32[32,128]{1,0:T(8,128)} %bitcast.15, f32[32,128]{1,0:T(8,128)} %bitcast.16, f32[2,128]{1,0:T(2,128)} %multiply_bitcast_fusion.pos_ref), custom_call_target="tpu_custom_call" | custom-call | tf_op jit(solution)/shard_map/exchange_sums/pallas_call | solution.py:251
  97.6 2.0 broadcast_in_dim.8.a_ref
  99.6 49.4 %grad_pass.1 = (f32[2048,768]{1,0:T(8,128)}, f32[16,768,256]{2,1,0:T(8,128)}) custom-call(bf16[2048,768]{1,0:T(8,128)(2,1)} %get-tuple-element.19.img_ref, bf16[4096,768]{1,0:T(8,128)(2,1)} %get-tuple-element.20.txt_ref, f32[2048,4096]{1,0:T(8,128)} %get-tuple-element.21.e_ref, f32[2048,128]{1,0:T(8,128)} %broadcast_in_dim.8.a_ref, f32[1,4096]{1,0:T(1,128)} %bitcast.20), custom_call_target="tpu_custom_call" | custom-call | flops 25769803776 | bytes 33554432 | tf_op jit(solution)/shard_map/grad_pass/pallas_call | solution.py:323
  149.1 56.5 %reduce_blocks.1 = (f32[256,768]{1,0:T(8,128)}, f32[768,256]{1,0:T(8,128)}, f32[8,128]{1,0:T(8,128)}) custom-call(f32[8,256,768]{2,1,0:T(8,128)} %bitcast.14, f32[16,768,256]{2,1,0:T(8,128)} %get-tuple-element.29.dtxt_ref, f32[8,128]{1,0:T(8,128)} %get-tuple-element.30.part_ref), custom_call_target="tpu_custom_call" | custom-call | tf_op jit(solution)/shard_map/reduce_blocks/pallas_call | solution.py:481
  205.6 0.8 slice_reduce_fusion
  206.4 0.6 fusion.1
  207.0 1.9 multiply_convert_fusion.1
  208.9 1.2 fusion
  210.1 0.9 copy.7

commit v2 on v1

--- a/solution.py
+++ b/solution.py
@@ -53,9 +53,10 @@
         self.copies.append(copy)
         return copy
 
-    def finish(self):
+    def finish(self, skip=()):
         for copy in self.copies:
-            copy.wait_send()
+            if not any(copy is other for other in skip):
+                copy.wait_send()
 
 
 def greet(peers):
@@ -143,7 +144,7 @@
 CM = 256
 
 
-def pass1_kernel(scale_ref, img_ref, txt_ref, e_ref, rs_ref, rl_ref, cs_ref, cl_ref):
+def pass1_kernel(scale_ref, img_ref, txt_ref, e_ref, rs_ref, rl_ref, cs_ref, cl_ref, imgt_ref):
     j = pl.program_id(0)
     scale = scale_ref[0]
     rows = img_ref.shape[0]
@@ -152,6 +153,8 @@
     def _():
         rs_ref[...] = jnp.zeros_like(rs_ref)
         rl_ref[...] = jnp.zeros_like(rl_ref)
+        for i in range(rows // 256):
+            imgt_ref[:, i * 256:(i + 1) * 256] = img_ref[i * 256:(i + 1) * 256, :].T
 
     cs_ref[...] = jnp.zeros_like(cs_ref)
     cl_ref[...] = jnp.zeros_like(cl_ref)
@@ -186,12 +189,12 @@
         grid=(n // BN,),
         out_shape=[jax.ShapeDtypeStruct((m, n), F32), jax.ShapeDtypeStruct((m, 128), F32),
                    jax.ShapeDtypeStruct((m, 128), F32), jax.ShapeDtypeStruct((8, n), F32),
-                   jax.ShapeDtypeStruct((8, n), F32)],
+                   jax.ShapeDtypeStruct((8, n), F32), jax.ShapeDtypeStruct((d, m), BF16)],
         in_specs=[pl.BlockSpec(memory_space=pltpu.SMEM), pl.BlockSpec((m, d), whole),
                   pl.BlockSpec((BN, d), lambda j: (j, 0))],
         out_specs=[pl.BlockSpec((m, BN), lambda j: (0, j)), pl.BlockSpec((m, 128), whole),
                    pl.BlockSpec((m, 128), whole), pl.BlockSpec((8, BN), lambda j: (0, j)),
-                   pl.BlockSpec((8, BN), lambda j: (0, j))],
+                   pl.BlockSpec((8, BN), lambda j: (0, j)), pl.BlockSpec((d, m), whole)],
         compiler_params=pltpu.CompilerParams(dimension_semantics=("arbitrary",), vmem_limit_bytes=VMEM_LIMIT),
         cost_estimate=pl.CostEstimate(flops=2 * m * n * d, bytes_accessed=4 * m * n, transcendentals=m * n),
         name="logits_pass")(scale, img_all, txt_all)
@@ -260,129 +263,64 @@
         name="exchange_sums")(rs, rl, cs, cl, pos)
 
 
-CI = 512
-
-
-def pass2_kernel(inv, n, img_ref, txt_ref, e_ref, a_ref, b_ref, dimg_ref, dtxt_ref, gb_ref, imgt_ref):
-    j = pl.program_id(0)
-    rows, d = img_ref.shape
-
-    @pl.when(j == 0)
-    def _():
-        for i in range(rows // 256):
-            imgt_ref[:, i * 256:(i + 1) * 256] = img_ref[i * 256:(i + 1) * 256, :].T
-
-    b = b_ref[...]
-
-    def grad_step(i, carry):
-        at = pl.ds(pl.multiple_of(i * CM, CM), CM)
-        a = a_ref[at, :]
-        for q in range(BN // 128):
-            lanes = slice(q * 128, (q + 1) * 128)
-            gb_ref[at, lanes] = (e_ref[at, lanes] * (a + b[:, lanes])).astype(BF16)
-        return carry
-
-    lax.fori_loop(0, rows // CM, grad_step, 0)
-
-    @pl.when(j == 0)
-    def _():
-        diag = lax.broadcasted_iota(jnp.int32, (n, n), 0) == lax.broadcasted_iota(jnp.int32, (n, n), 1)
-        for q in range(n // 128):
-            lanes = slice(q * 128, (q + 1) * 128)
-            grad = e_ref[0:n, lanes] * (a_ref[0:n, :] + b[:, lanes])
-            gb_ref[0:n, lanes] = (grad - jnp.where(diag[:, lanes], 2.0 * inv, 0.0)).astype(BF16)
-
-    def txt_step(i, carry):
-        at = pl.ds(pl.multiple_of(i * 256, 256), 256)
-        part = jnp.dot(imgt_ref[at, :], gb_ref[...], preferred_element_type=F32)
-        for q in range(BN // n):
-            dtxt_ref[q, at, :] = part[:, q * n:(q + 1) * n]
-        return carry
-
-    lax.fori_loop(0, d // 256, txt_step, 0)
-
-    def img_step(first, i, carry):
-        at = pl.ds(pl.multiple_of(i * CI, CI), CI)
-        part = jnp.dot(gb_ref[at, :], txt_ref[...], preferred_element_type=F32)
-        dimg_ref[at, :] = part if first else dimg_ref[at, :] + part
-        return carry
-
-    @pl.when(j == 0)
-    def _():
-        lax.fori_loop(0, rows // CI, functools.partial(img_step, True), 0)
-
-    @pl.when(j > 0)
-    def _():
-        lax.fori_loop(0, rows // CI, functools.partial(img_step, False), 0)
-
-
-def pass2(inv, n, img_all, txt_all, e, a, b):
-    m, d = img_all.shape
-    nt = txt_all.shape[0]
-    whole = lambda j: (0, 0)
-    return pl.pallas_call(
-        functools.partial(pass2_kernel, inv, n),
-        grid=(nt // BN,),
-        out_shape=[jax.ShapeDtypeStruct((m, d), F32), jax.ShapeDtypeStruct((nt // n, d, n), F32)],
-        in_specs=[pl.BlockSpec((m, d), whole), pl.BlockSpec((BN, d), lambda j: (j, 0)),
-                  pl.BlockSpec((m, BN), lambda j: (0, j)), pl.BlockSpec((m, 128), whole),
-                  pl.BlockSpec((1, BN), lambda j: (0, j))],
-        out_specs=[pl.BlockSpec((m, d), whole), pl.BlockSpec((BN // n, d, n), lambda j: (j, 0, 0))],
-        scratch_shapes=[pltpu.VMEM((m, BN), BF16), pltpu.VMEM((d, m), BF16)],
-        compiler_params=pltpu.CompilerParams(dimension_semantics=("arbitrary",), vmem_limit_bytes=VMEM_LIMIT),
-        cost_estimate=pl.CostEstimate(flops=4 * m * nt * d, bytes_accessed=4 * m * nt, transcendentals=0),
-        name="grad_pass")(img_all, txt_all, e, a, b)
-
-
+ICUT = 144
+TCUT = 432
+ORDER = (6, 5, 7, 2, 1, 4, 3, 0)
+KC = 512
 N_REDUCE = 8 + 2 * (4 + 18 + 1) + 22
 
 
 class Ring:
-    def __init__(self, net, acc, buf, ybuf, rows, cut, plus, minus, pair):
-        self.net, self.acc, self.buf, self.ybuf = net, acc, buf, ybuf
-        self.cut, self.rows = cut, rows
+    def __init__(self, net, acc, buf, cut, plus, minus, pair):
+        self.net, self.acc, self.buf = net, acc, buf
+        self.cut, self.rows = cut, acc.shape[1]
         self.plus, self.minus, self.pair = plus, minus, pair
-        self.streams = {}
-
-    def pair_first(self):
-        lo, size = self.cut, self.rows - self.cut
-        self.early = {d: self.net.send(self.acc.at[4 + d, pl.ds(lo, size)], self.ybuf.at[d, pl.ds(lo, size)], self.pair)
-                      for d in (2, 1, 3, 0)}
-
-    def pair_add(self):
-        lo, size = self.cut, self.rows - self.cut
-        for d in (2, 1, 3, 0):
-            self.early[d].wait_recv()
-            self.acc[d, lo:lo + size] += self.ybuf[d, lo:lo + size]
-
-    def start(self, name, dy, lo, size):
-        h, b = size // 2, 4 * dy
-        acc, buf, send = self.acc, self.buf, self.net.send
-        s = dict(lo=lo, h=h, b=b)
-        h0, h1 = pl.ds(lo, h), pl.ds(lo + h, h)
-        s["a_plus"] = send(acc.at[b + 2, h0], buf.at[b + 2, h0], self.plus)
-        s["a_minus"] = send(acc.at[b + 2, h1], buf.at[b + 2, h1], self.minus)
-        s["b_plus_h1"] = send(acc.at[b + 1, h1], buf.at[b + 3, h1], self.plus)
-        s["b_minus_h0"] = send(acc.at[b + 3, h0], buf.at[b + 1, h0], self.minus)
-        self.streams[name] = s
-
-    def middle(self, name):
-        s = self.streams[name]
-        acc, buf, send = self.acc, self.buf, self.net.send
-        lo, h, b = s["lo"], s["h"], s["b"]
-        h0, h1 = pl.ds(lo, h), pl.ds(lo + h, h)
-        s["a_plus"].wait_recv()
-        acc[b + 1, lo:lo + h] += buf[b + 2, lo:lo + h]
-        s["b_plus_h0"] = send(acc.at[b + 1, h0], buf.at[b + 3, h0], self.plus)
-        s["a_minus"].wait_recv()
-        acc[b + 3, lo + h:lo + 2 * h] += buf[b + 2, lo + h:lo + 2 * h]
-        s["b_minus_h1"] = send(acc.at[b + 3, h1], buf.at[b + 1, h1], self.minus)
+        self.early, self.streams = {}, {}
+
+    def pair_send(self, d):
+        at = pl.ds(self.cut, self.rows - self.cut)
+        self.early[d] = self.net.send(self.acc.at[4 + d, at], self.buf.at[4 + d, at], self.pair)
+
+    def pair_add(self, d):
+        self.early[d].wait_recv()
+        self.acc[d, self.cut:] += self.buf[4 + d, self.cut:]
+
+    def where(self, name):
+        if name == 2:
+            return 0, self.cut, (self.rows - self.cut) // 2
+        return 4 * name, 0, self.cut // 2
+
+    def send(self, name, key, slot, half, to_slot, peer):
+        _, lo, h = self.where(name)
+        at = pl.ds(lo + half * h, h)
+        self.streams[name, key] = self.net.send(self.acc.at[slot, at], self.buf.at[to_slot, at], peer)
+
+    def far(self, name):
+        b, _, _ = self.where(name)
+        self.send(name, "a+", b + 2, 0, b + 2, self.plus)
+        self.send(name, "a-", b + 2, 1, b + 2, self.minus)
+
+    def plain_plus(self, name):
+        b, _, _ = self.where(name)
+        self.send(name, "b+1", b + 1, 1, b + 3, self.plus)
+
+    def plain_minus(self, name):
+        b, _, _ = self.where(name)
+        self.send(name, "b-0", b + 3, 0, b + 1, self.minus)
+
+    def mid(self, name):
+        b, lo, h = self.where(name)
+        self.streams[name, "a+"].wait_recv()
+        self.acc[b + 1, lo:lo + h] += self.buf[b + 2, lo:lo + h]
+        self.send(name, "b+0", b + 1, 0, b + 3, self.plus)
+        self.streams[name, "a-"].wait_recv()
+        self.acc[b + 3, lo + h:lo + 2 * h] += self.buf[b + 2, lo + h:lo + 2 * h]
+        self.send(name, "b-1", b + 3, 1, b + 1, self.minus)
 
     def end(self, name):
-        s = self.streams[name]
-        lo, h, b = s["lo"], s["h"], s["b"]
-        for key in ("b_plus_h1", "b_minus_h0", "b_plus_h0", "b_minus_h1"):
-            s[key].wait_recv()
+        b, lo, h = self.where(name)
+        for key in ("b+1", "b-0", "b+0", "b-1"):
+            self.streams[name, key].wait_recv()
         self.acc[b, lo:lo + 2 * h] += self.buf[b + 1, lo:lo + 2 * h] + self.buf[b + 3, lo:lo + 2 * h]
 
     def pair_last(self):
@@ -393,104 +331,222 @@
         self.late.wait_recv()
         self.acc[0, 0:self.cut] += self.buf[0, 0:self.cut]
 
-
-def reduce_kernel(dimg_ref, dtxt_ref, part_ref, img_out, txt_out, part_out, iacc, tacc, ibuf, tbuf, iy, ty, dbuf, pa, pb,
-                  psum, local_sems, send_sems, recv_sems):
+    def ready(self, step):
+        if step == 0:
+            self.pair_send(2)
+            self.far(1)
+        elif step == 1:
+            self.pair_send(1)
+            self.plain_plus(1)
+        elif step == 2:
+            self.pair_send(3)
+            self.plain_minus(1)
+            self.mid(1)
+        elif step == 3:
+            self.far(0)
+            self.pair_add(2)
+            self.far(2)
+        elif step == 4:
+            self.plain_plus(0)
+            self.pair_add(1)
+            self.plain_plus(2)
+        elif step == 5:
+            self.pair_send(0)
+            self.end(1)
+            self.pair_last()
+        elif step == 6:
+            self.plain_minus(0)
+            self.pair_add(3)
+            self.plain_minus(2)
+            self.mid(0)
+
+    def close(self):
+        self.pair_add(0)
+        self.end(0)
+        self.pair_end()
+        self.end(2)
+
+
+def grads_kernel(inv, imgt_hbm, txt_hbm, e_hbm, a_ref, b_ref, part_ref, img_out, txt_out, part_out,
+                 imgt, txt, erow, ecol, gb0, gb1, arow, stage, iacc, tacc, ibuf, tbuf, dbuf, pa, pb, psum,
+                 local_sems, row_sems, col_sems, send_sems, recv_sems):
     g = Grid()
+    n = iacc.shape[1]
+    d = iacc.shape[2]
+    m = imgt.shape[1]
+    nt = txt.shape[0]
     img_offs = [(dy, dz) for dy in (0, 1) for dz in range(4) if (dy, dz) != (0, 0)]
     txt_offs = [(dc, dy, dx) for dc in (0, 1) for dy in (0, 1) for dx in range(4) if (dc, dy, dx) != (0, 0, 0)]
-    loads = {}
-    for k in (6, 2, 5, 1, 7, 3, 4, 0):
-        loads["t", k] = pltpu.make_async_copy(dtxt_ref.at[k], tacc.at[k], local_sems.at[k])
-        loads["i", k] = pltpu.make_async_copy(dimg_ref.at[k], iacc.at[k], local_sems.at[8 + k])
-        loads["t", k].start()
-        loads["i", k].start()
+
+    def row_load(step):
+        k = ORDER[step]
+        return pltpu.make_async_copy(e_hbm.at[pl.ds(k * n, n)], erow.at[step % 2], row_sems.at[step % 2])
+
+    def col_load(step, side):
+        k = ORDER[step] + 8 * side
+        return pltpu.make_async_copy(e_hbm.at[:, pl.ds(k * n, n)], ecol.at[side], col_sems.at[side])
+
+    load_imgt = pltpu.make_async_copy(imgt_hbm, imgt, local_sems.at[0])
+    load_txt = pltpu.make_async_copy(txt_hbm, txt, local_sems.at[1])
+    cols = {}
+    cols[0, 1] = col_load(0, 1)
+    cols[0, 1].start()
+    load_imgt.start()
+    rows = {0: row_load(0)}
+    rows[0].start()
+    load_txt.start()
+    cols[0, 0] = col_load(0, 0)
+    cols[0, 0].start()
+    for i in range(m // 128):
+        arow[i * 128:(i + 1) * 128, :] = jnp.broadcast_to(a_ref[i:i + 1, :], (128, 128)).T
     greet([g.img_peer(*o) for o in img_offs] + [g.txt_peer(*o) for o in txt_offs])
     net = Net(send_sems, recv_sems)
     core = g.txt_peer(1, 0, 0)
-    cross = {k: net.send(dtxt_ref.at[8 + k], dbuf.at[k], core) for k in (6, 5, 7, 4, 2, 1, 3, 0)}
     ia = g.z * 2 + g.y % 2
     ib = (g.x * 2 + g.y // 2) * 2 + g.c
     scal_a = [net.send(part_ref, pa.at[ia], g.img_peer(*o)) for o in img_offs]
     pa[ia] = part_ref[...]
-
-    img = Ring(net, iacc, ibuf, iy, iacc.shape[1], ICUT, g.img_peer(0, 1), g.img_peer(0, 3), g.img_peer(1, 0))
-    txt = Ring(net, tacc, tbuf, ty, tacc.shape[1], TCUT, g.txt_peer(0, 0, 1), g.txt_peer(0, 0, 3), g.txt_peer(0, 1, 0))
-    for k in (6, 5, 7, 4):
-        loads["i", k].wait()
-    img.pair_first()
-    img.start("1", 1, 0, img.cut)
-    for k in (2, 1, 3, 0):
-        loads["i", k].wait()
-    img.start("0", 0, 0, img.cut)
-    for k in (6, 5, 7, 4):
-        loads["t", k].wait()
+    img = Ring(net, iacc, ibuf, ICUT, g.img_peer(0, 1), g.img_peer(0, 3), g.img_peer(1, 0))
+    txr = Ring(net, tacc, tbuf, TCUT, g.txt_peer(0, 0, 1), g.txt_peer(0, 0, 3), g.txt_peer(0, 1, 0))
+
+    def minus_diag(grad, q):
+        r = lax.broadcasted_iota(jnp.int32, (n, 128), 0)
+        c = lax.broadcasted_iota(jnp.int32, (n, 128), 1) + q * 128
+        head = grad[:n] - jnp.where(r == c, 2.0 * inv, 0.0)
+        return head if grad.shape[0] == n else jnp.concatenate([head, grad[n:]], axis=0)
+
+    def col_slot(k, e_ref, out_ref):
+        b = [b_ref[2 * k + q:2 * k + q + 1, :] for q in range(n // 128)]
+
+        def grad(i, to, diag=False):
+            at = pl.ds(i * KC, KC)
+            a = arow[at, :]
+            for q in range(n // 128):
+                lanes = slice(q * 128, (q + 1) * 128)
+                v = e_ref[at, lanes] * (a + b[q])
+                if diag:
+                    v = minus_diag(v, q)
+                to[:, lanes] = v.astype(BF16)
+
+        grad(0, gb0[0], diag=k == 0)
+        out_ref[...] = jnp.zeros_like(out_ref)
+        count = m // KC
+
+        def body(it, carry):
+            for half, (now, later) in enumerate(((gb0[0], gb0[1]), (gb0[1], gb0[0]))):
+                i = 2 * it + half
+                at = pl.ds(pl.multiple_of(i * KC, KC), KC)
+                out_ref[...] += jnp.dot(imgt[:, at], now[...], preferred_element_type=F32)
+                grad_dyn((i + 1) % count, later)
+            return carry
+
+        def grad_dyn(i, to):
+            at = pl.ds(pl.multiple_of(i * KC, KC), KC)
+            a = arow[at, :]
+            for q in range(n // 128):
+                lanes = slice(q * 128, (q + 1) * 128)
+                to[:, lanes] = (e_ref[at, lanes] * (a + b[q])).astype(BF16)
+
+        lax.fori_loop(0, count // 2, body, 0)
+
+    def row_slot(k, e_ref, out_ref):
+        count = nt // KC
+
+        def grad(i, to, diag=False):
+            for q in range(KC // 128):
+                lanes = pl.ds(pl.multiple_of(i * KC + q * 128, 128), 128)
+                v = e_ref[:, lanes] * (arow[k * n:(k + 1) * n, :] + b_ref[pl.ds(i * (KC // 128) + q, 1), :])
+                if diag and q < n // 128:
+                    v = minus_diag(v, q)
+                to[:, q * 128:(q + 1) * 128] = v.astype(BF16)
+
+        grad(0, gb1[0], diag=k == 0)
+        out_ref[...] = jnp.zeros_like(out_ref)
+
+        def body(it, carry):
+            for half, (now, later) in enumerate(((gb1[0], gb1[1]), (gb1[1], gb1[0]))):
+                i = 2 * it + half
+                at = pl.ds(pl.multiple_of(i * KC, KC), KC)
+                out_ref[...] += jnp.dot(now[...], txt[at, :], preferred_element_type=F32)
+                grad((i + 1) % count, later)
+            return carry
+
+        lax.fori_loop(0, count // 2, body, 0)
+
+    cross = {}
+    for step, k in enumerate(ORDER):
+        cols[step, 1].wait()
+        if step == 0:
+            load_imgt.wait()
+        if step >= 2:
+            cross[ORDER[step - 2]].wait_send()
+        col_slot(8 + k, ecol.at[1], stage.at[step % 2])
+        cross[k] = net.send(stage.at[step % 2], dbuf.at[k], core)
+        if step + 1 < len(ORDER):
+            cols[step + 1, 1] = col_load(step + 1, 1)
+            cols[step + 1, 1].start()
+            rows[step + 1] = row_load(step + 1)
+            rows[step + 1].start()
+        rows[step].wait()
+        if step == 0:
+            load_txt.wait()
+        row_slot(k, erow.at[step % 2], iacc.at[k])
+        img.ready(step)
+        cols[step, 0].wait()
+        col_slot(k, ecol.at[0], tacc.at[k])
+        if step + 1 < len(ORDER):
+            cols[step + 1, 0] = col_load(step + 1, 0)
+            cols[step + 1, 0].start()
         cross[k].wait_recv()
         tacc[k] += dbuf[k]
-    txt.pair_first()
-    txt.start("1", 1, 0, txt.cut)
-    for k in (2, 1, 3, 0):
-        loads["t", k].wait()
-        cross[k].wait_recv()
-        tacc[k] += dbuf[k]
-    txt.start("0", 0, 0, txt.cut)
-    for copy in scal_a:
-        copy.wait_recv()
-    total = pa[0]
-    for k in range(1, 8):
-        total += pa[k]
-    psum[...] = total
-    scal_b = [net.send(psum, pb.at[ib], g.txt_peer(*o)) for o in txt_offs]
-    pb[ib] = total
-    for r in (img, txt):
-        r.middle("1")
-    for r in (img, txt):
-        r.end("1")
-        r.pair_last()
-        r.middle("0")
-    for r in (img, txt):
-        r.pair_add()
-        r.start("2", 0, r.cut, r.rows - r.cut)
+        txr.ready(step)
+        if step == 1:
+            for copy in scal_a:
+                copy.wait_recv()
+            total = pa[0]
+            for q in range(1, 8):
+                total += pa[q]
+            psum[...] = total
+            scal_b = [net.send(psum, pb.at[ib], g.txt_peer(*o)) for o in txt_offs]
+            pb[ib] = total
+    for r in (img, txr):
+        r.mid(2)
     for copy in scal_b:
         copy.wait_recv()
     total = pb[0]
     for k in range(1, 16):
         total += pb[k]
     part_out[...] = total
-    for r in (img, txt):
-        r.end("0")
-    for r in (img, txt):
-        r.middle("2")
-    for r in (img, txt):
-        r.pair_end()
-    for r in (img, txt):
-        r.end("2")
+    for r in (img, txr):
+        r.close()
     img_out[...] = iacc[0]
     txt_out[...] = tacc[0]
-    net.finish()
-
-
-ICUT = 144
-TCUT = 432
-
-
-def reduce_scatter(dimg, dtxt, part):
-    _, n, d = dimg.shape
+    net.finish(skip=[cross[k] for k in ORDER[:-2]])
+
+
+def grads(inv, imgt, txt_all, e, a, b, part):
+    d, m = imgt.shape
+    nt = txt_all.shape[0]
+    n = m // 8
     vmem = pl.BlockSpec(memory_space=pltpu.VMEM)
     hbm = pl.BlockSpec(memory_space=pl.ANY)
+    dma = pltpu.SemaphoreType.DMA
     return pl.pallas_call(
-        reduce_kernel,
+        functools.partial(grads_kernel, inv),
         out_shape=[jax.ShapeDtypeStruct((n, d), F32), jax.ShapeDtypeStruct((d, n), F32),
                    jax.ShapeDtypeStruct((8, 128), F32)],
-        in_specs=[hbm, hbm, vmem],
+        in_specs=[hbm, hbm, hbm, vmem, vmem, vmem],
         out_specs=[vmem] * 3,
-        scratch_shapes=[pltpu.VMEM((8, n, d), F32), pltpu.VMEM((8, d, n), F32), pltpu.VMEM((8, n, d), F32),
-                        pltpu.VMEM((8, d, n), F32), pltpu.VMEM((4, n, d), F32), pltpu.VMEM((4, d, n), F32),
+        scratch_shapes=[pltpu.VMEM((d, m), BF16), pltpu.VMEM((nt, d), BF16), pltpu.VMEM((2, n, nt), F32),
+                        pltpu.VMEM((2, m, n), F32), [pltpu.VMEM((KC, n), BF16)] * 2, [pltpu.VMEM((n, KC), BF16)] * 2,
+                        pltpu.VMEM((m, 128), F32), pltpu.VMEM((2, d, n), F32), pltpu.VMEM((8, n, d), F32),
+                        pltpu.VMEM((8, d, n), F32), pltpu.VMEM((8, n, d), F32), pltpu.VMEM((8, d, n), F32),
                         pltpu.VMEM((8, d, n), F32), pltpu.VMEM((8, 8, 128), F32), pltpu.VMEM((16, 8, 128), F32),
-                        pltpu.VMEM((8, 128), F32), pltpu.SemaphoreType.DMA((16,)),
-                        pltpu.SemaphoreType.DMA((N_REDUCE,)), pltpu.SemaphoreType.DMA((N_REDUCE,))],
+                        pltpu.VMEM((8, 128), F32), dma((2,)), dma((2,)), dma((2,)), dma((N_REDUCE,)),
+                        dma((N_REDUCE,))],
         compiler_params=pltpu.CompilerParams(collective_id=2, has_side_effects=True, vmem_limit_bytes=VMEM_LIMIT),
-        name="reduce_blocks")(dimg, dtxt, part)
+        cost_estimate=pl.CostEstimate(flops=4 * m * nt * d, bytes_accessed=8 * m * nt, transcendentals=0),
+        name="grads_reduce")(imgt, txt_all, e, a, b, part)
 
 
 def solution(mesh):
@@ -503,13 +559,11 @@
         scale = jnp.exp(log_scale)
         pos = scale * jnp.sum(img_loc.astype(F32) * txt_loc.astype(F32), axis=1)
         img_all, txt_all = gather(img_loc, txt_loc)
-        e, rs, rl, cs, cl = pass1(scale.reshape(1), img_all, txt_all)
+        e, rs, rl, cs, cl, imgt = pass1(scale.reshape(1), img_all, txt_all)
         rows = lambda v: jnp.sum(v, axis=1).reshape(-1, 128)
         cols = lambda v: jnp.sum(v, axis=0).reshape(-1, 128)
         a, b, part = exchange_sums(inv, rows(rs), rows(rl), cols(cs), cols(cl), pos.reshape(-1, 128))
-        a_rows = jnp.broadcast_to(a.reshape(-1, 1), (8 * n, 128))
-        dimg, dtxt = pass2(inv, n, img_all, txt_all, e, a_rows, b.reshape(1, -1))
-        img_sum, txt_sum, tot = reduce_scatter(dimg.reshape(8, n, d), dtxt, part)
+        img_sum, txt_sum, tot = grads(inv, imgt, txt_all, e, a, b, part)
         d_img = (scale * img_sum).astype(BF16)
         d_txt = (scale * txt_sum).T.astype(BF16)
         tot = jnp.sum(tot[0:2], axis=1)

time: 212 us -> 169 us (0.80)
  Pallas kernels: 193 us -> 154 us
    pallas_call x2 -> x1, Pallas kernels: 106 us -> 64.9 us  [grads(): pl.pallas_call(functools.partial(grads_kernel, inv), out_shape=[jax.Shape...]
where the time goes in v2:
time: 169 us
  Pallas kernels  154 us (91%)
  other arithmetic  12.1 us (7%)
    pallas_call x1, Pallas kernels, grads(): pl.pallas_call(functools.partial(grads_kernel, inv), out_shape=[jax.Shape...  64.9 us
    pallas_call x1, Pallas kernels, gather(): pl.pallas_call(functools.partial(gather_kernel, n), out_shape=[jax.ShapeD...  39.8 us
    pallas_call x1, Pallas kernels, pass1(): pl.pallas_call(pass1_kernel, grid=(n // BN,), out_shape=[jax.ShapeDtypeSt...  38.4 us
    pallas_call x1, Pallas kernels, exchange_sums(): pl.pallas_call(functools.partial(sums_kernel, inv), out_shape=[jax.ShapeD...  10.8 us
    reduce_sum x2, other arithmetic, local_tile(): rows = lambda v: jnp.sum(v, axis=1).reshape(-1, 128)  4.33 us

profile of v2, /device:TPU:1, one launch (start us, length us, event | category | flops | bytes accessed | tf_op | source)
XLA Modules:
  0.0 168.9 jit_solution(207165614202218135)
XLA Ops:
  1.3 39.8 %gather_blocks.1 = (bf16[2048,768]{1,0:T(8,128)(2,1)}, bf16[4096,768]{1,0:T(8,128)(2,1)}) custom-call(bf16[256,768]{1,0:T(8,128)(2,1)} %img_ref.1, bf16[256,768]{1,0:T(8,128)(2,1)} %txt_ref.1), custom_call_target="tpu_custom_call" | custom-call | tf_op jit(solution)/shard_map/gather_blocks/pallas_call | solution.py:132
  41.2 0.0 copy-start
  41.2 0.0 copy-start.1
  41.2 38.4 %logits_pass.1 = (f32[2048,4096]{1,0:T(8,128)}, f32[2048,128]{1,0:T(8,128)}, f32[2048,128]{1,0:T(8,128)}, f32[8,4096]{1,0:T(8,128)}, f32[8,4096]{1,0:T(8,128)}, /*index=5*/bf16[768,2048]{1,0:T(8,128)(2,1)}) custom-call(f32[1]{0:T(128)} %bitcast.scale_ref, bf16[2048,768]{1,0:T(8,128)(2,1)} %get-tuple-element.18.img_ref, ...), custom_call_target="tpu_custom_call" | custom-call | flops 12884901888 | bytes 33554432 | tf_op jit(solution)/shard_map/logits_pass/pallas_call | solution.py:187
  79.6 1.5 reduce_sum.56
  81.2 1.5 reduce_sum.57
  82.7 2.2 %reduce_sum.54 = f32[2048]{0:T(1024)} reduce(f32[2048,128]{1,0:T(8,128)} %get-tuple-element.22, f32[]{:T(128)} %constant.0.clone.1), dimensions={1}, to_apply=%region_0.0 | reduce | flops 260096 | bytes 1056772 | tf_op jit(solution)/shard_map/reduce_sum | solution.py:563
  84.9 2.2 %reduce_sum.55 = f32[2048]{0:T(1024)} reduce(f32[2048,128]{1,0:T(8,128)} %get-tuple-element.23, f32[]{:T(128)} %constant.0.clone.1), dimensions={1}, to_apply=%region_1.0 | reduce | flops 260096 | bytes 1056772 | tf_op jit(solution)/shard_map/reduce_sum | solution.py:563
  87.0 0.0 copy-done
  87.0 0.0 copy-done.1
  87.0 0.2 multiply_reduce_fusion
  87.2 0.6 multiply_bitcast_fusion.pos_ref
  87.8 10.8 %exchange_sums.1 = (f32[16,128]{1,0:T(8,128)}, f32[32,128]{1,0:T(8,128)}, f32[8,128]{1,0:T(8,128)}) custom-call(f32[16,128]{1,0:T(8,128)} %bitcast.13, f32[16,128]{1,0:T(8,128)} %bitcast.14, f32[32,128]{1,0:T(8,128)} %bitcast.11, f32[32,128]{1,0:T(8,128)} %bitcast.12, f32[2,128]{1,0:T(2,128)} %multiply_bitcast_fusion.pos_ref), custom_call_target="tpu_custom_call" | custom-call | tf_op jit(solution)/shard_map/exchange_sums/pallas_call | solution.py:254
  98.6 64.9 %grads_reduce.1 = (f32[256,768]{1,0:T(8,128)}, f32[768,256]{1,0:T(8,128)}, f32[8,128]{1,0:T(8,128)}) custom-call(bf16[768,2048]{1,0:T(8,128)(2,1)} %get-tuple-element.20.imgt_hbm, bf16[4096,768]{1,0:T(8,128)(2,1)} %get-tuple-element.19.txt_ref.txt_hbm, f32[2048,4096]{1,0:T(8,128)} %get-tuple-element.21.e_hbm, f32[16,128]{1,0:T(8,128)} %get-tuple-element.26.a_ref, ...), custom_call_target="tpu_custom_call" | custom-call | flops 25769803776 | bytes 67108864 | tf_op jit(solution)/shard_map/grads_reduce/pallas_call | solution.py:534
  163.5 1.2 fusion
  164.7 0.9 copy.7
  165.6 1.9 %multiply_convert_fusion.1 = bf16[256,768]{1,0:T(8,128)(2,1)} fusion(f32[256,768]{1,0:T(8,128)} %get-tuple-element.30, f32[]{:T(128)} %exp.3), kind=kLoop, calls=%fused_computation.1 | loop fusion | flops 393216 | bytes 1179652 | tf_op jit(solution)/shard_map/convert_element_type | solution.py:567
  167.6 0.8 slice_reduce_fusion
  168.4 0.6 fusion.1
Async XLA Ops:
  41.2 45.9 %copy-start = (bf16[256,768]{1,0:T(8,128)(2,1)S(1)}, bf16[256,768]{1,0:T(8,128)(2,1)}, u32[]{:S(2)}) copy-start(bf16[256,768]{1,0:T(8,128)(2,1)} %img_ref.1) | copy-start | bytes 1179652
  41.2 45.9 %copy-start.1 = (bf16[256,768]{1,0:T(8,128)(2,1)S(1)}, bf16[256,768]{1,0:T(8,128)(2,1)}, u32[]{:S(2)}) copy-start(bf16[256,768]{1,0:T(8,128)(2,1)} %txt_ref.1) | copy-start | bytes 1179652

commit v3 on v2

v3 whole, which is shorter than its diff:
```python
import functools

import jax
import jax.numpy as jnp
from jax import lax
from jax.experimental import pallas as pl
from jax.experimental.pallas import tpu as pltpu
from jax.sharding import PartitionSpec as P

MESH = pl.DeviceIdType.MESH
F32 = jnp.float32
BF16 = jnp.bfloat16
VMEM_LIMIT = 64_000_000


class Grid:
    def __init__(self):
        row = lax.axis_index("row")
        self.c = lax.axis_index("col")
        self.z = row // 16
        self.y = (row // 4) % 4
        self.x = row % 4

    def dev(self, z, y, x, c):
        return {"row": (z * 4 + y) * 4 + x, "col": c}

    def y_a(self):
        return self.y + 1 - 2 * (self.y % 2)

    def y_b(self):
        return 3 - self.y

    def img_peer(self, dy, dz):
        y = self.y_a() if dy else self.y
        return self.dev((self.z + dz) % 4, y, self.x, self.c)

    def txt_peer(self, dc, dy, dx):
        y = self.y_b() if dy else self.y
        c = 1 - self.c if dc else self.c
        return self.dev(self.z, y, (self.x + dx) % 4, c)


class Net:
    def __init__(self, send_sems, recv_sems):
        self.send_sems, self.recv_sems, self.copies = send_sems, recv_sems, []

    def send(self, src, dst, peer):
        i = len(self.copies)
        copy = pltpu.make_async_remote_copy(
            src_ref=src, dst_ref=dst, send_sem=self.send_sems.at[i], recv_sem=self.recv_sems.at[i],
            device_id=peer, device_id_type=MESH)
        copy.start()
        self.copies.append(copy)
        return copy

    def finish(self, skip=()):
        for copy in self.copies:
            if not any(copy is other for other in skip):
                copy.wait_send()


def greet(peers):
    barrier = pltpu.get_barrier_semaphore()
    for peer in peers:
        pl.semaphore_signal(barrier, inc=1, device_id=peer, device_id_type=MESH)
    pl.semaphore_wait(barrier, len(peers))


def neighbours(g):
    return [g.img_peer(0, 1), g.img_peer(0, 3), g.img_peer(1, 0), g.txt_peer(0, 0, 1), g.txt_peer(0, 0, 3),
            g.txt_peer(0, 1, 0), g.txt_peer(1, 0, 0)]


POS = {0: 0, 4: 1, 3: 2, 1: 3, 2: 4, 7: 5, 5: 6, 6: 7}
N_FORWARD = 2 * 18 + 9 + 22


class Gather:
    def __init__(self, net, own, dst, plus, minus, pair):
        self.net, self.own, self.dst = net, own, dst
        self.n = own.shape[0]
        self.plus, self.minus, self.pair = plus, minus, pair
        self.got = {}

    def half(self, k, side):
        h = self.n // 2
        return self.dst.at[POS[k], pl.ds(side * h, h)]

    def send(self, key, src, k, side, peer):
        self.got[key, side] = self.net.send(src, self.half(k, side), peer)

    def first(self):
        h = self.n // 2
        own = [self.own.at[pl.ds(side * h, h)] for side in (0, 1)]
        for side in (0, 1):
            self.send("p0", own[side], 3, side, self.plus)
            self.send("m0", own[1 - side], 1, 1 - side, self.minus)
            self.send("y0", own[side], 4, side, self.pair)

    def wait(self, *keys):
        for key in keys:
            self.got[key].wait_recv()

    def far(self, dy):
        self.wait(("p%d" % dy, 0))
        self.send("f%d" % dy, self.half(4 * dy + 3, 0), 4 * dy + 2, 0, self.plus)
        self.wait(("m%d" % dy, 1))
        self.send("f%d" % dy, self.half(4 * dy + 1, 1), 4 * dy + 2, 1, self.minus)

    def second(self):
        self.wait(("y0", 0), ("y0", 1))
        for side in (0, 1):
            self.send("p1", self.half(4, side), 7, side, self.plus)
            self.send("m1", self.half(4, 1 - side), 5, 1 - side, self.minus)


def forward_kernel(inv, scale_ref, img_ref, txt_ref, e_out, imgt_out, txt_out, a_ref, b_ref, part_ref,
                   img_all, txt_all, imgt, d0, d1, s0, s1, rs, rl, cs, cl, rsum, csum, rbuf, cbuf,
                   e_sems, t_sems, i_sems, own_sems, send_sems, recv_sems):
    g = Grid()
    n, d = img_ref.shape
    scale = scale_ref[0]
    img_offs = [(dy, dz) for dy in (0, 1) for dz in range(4) if (dy, dz) != (0, 0)]
    txt_offs = [(dc, dy, dx) for dc in (0, 1) for dy in (0, 1) for dx in range(4) if (dc, dy, dx) != (0, 0, 0)]
    own = [pltpu.make_async_copy(img_ref, img_all.at[0], own_sems.at[0]),
           pltpu.make_async_copy(txt_ref, txt_all.at[0], own_sems.at[1])]
    for copy in own:
        copy.start()
    greet([g.img_peer(*o) for o in img_offs] + [g.txt_peer(*o) for o in txt_offs])
    net = Net(send_sems, recv_sems)
    core = g.txt_peer(1, 0, 0)
    img = Gather(net, img_ref, img_all, g.img_peer(0, 1), g.img_peer(0, 3), g.img_peer(1, 0))
    txt = Gather(net, txt_ref, txt_all, g.txt_peer(0, 0, 1), g.txt_peer(0, 0, 3), g.txt_peer(0, 1, 0))
    img.first()
    txt.first()
    cross = {0: net.send(txt_ref, txt_all.at[8], core)}
    saves = []

    def save_txt(p):
        copy = pltpu.make_async_copy(txt_all.at[p], txt_out.at[pl.ds(p * n, n)], t_sems.at[p])
        copy.start()
        saves.append(copy)

    def got_txt(*slots):
        for k in slots:
            p = POS[k]
            cross[p] = net.send(txt_all.at[p], txt_all.at[8 + p], core)
            save_txt(p)

    def got_cross(*slots):
        for k in slots:
            cross[POS[k]].wait_recv()
            save_txt(8 + POS[k])

    def got_img(*slots):
        for k in slots:
            p = POS[k]
            imgt[p] = img_all[p].T
            copy = pltpu.make_async_copy(imgt.at[p], imgt_out.at[:, pl.ds(p * n, n)], i_sems.at[p])
            copy.start()
            saves.append(copy)

    dots, stage = (d0, d1), (s0, s1)

    def dot(i, k, buf):
        lhs = img_all[i]
        for side in (0, 1):
            dots[buf][side] = lax.dot_general(lhs, txt_all[8 * side + k], (((1,), (1,)), ((), ())),
                                              preferred_element_type=F32)

    def store(i, k, buf):
        return pltpu.make_async_copy(stage[buf], e_out.at[i, :, k], e_sems.at[buf])

    def finish_unit(i, k, buf, first=False):
        if not first:
            store(i, k, buf).wait()
        at = pl.ds(i * n, n) if isinstance(i, int) else pl.ds(pl.multiple_of(i * n, n), n)
        for blk in range(n // 32):
            lo = blk * 32
            rows = pl.ds(i * n + lo, 32) if isinstance(i, int) else pl.ds(pl.multiple_of(i * n + lo, 32), 32)
            racc, lacc = rs[rows, :], rl[rows, :]
            for side in (0, 1):
                logits = scale * dots[buf][side, lo:lo + 32, :]
                e = jnp.exp(logits)
                el = e * logits
                stage[buf][side, lo:lo + 32, :] = e
                for q in range(n // 128):
                    racc += e[:, q * 128:(q + 1) * 128]
                    lacc += el[:, q * 128:(q + 1) * 128]
                cs[8 * side + k] += jnp.sum(e.reshape(4, 8, n), axis=0)
                cl[8 * side + k] += jnp.sum(el.reshape(4, 8, n), axis=0)
            rs[rows, :] = racc
            rl[rows, :] = lacc
        store(i, k, buf).start()

    state = {"buf": 0, "unit": (0, 0)}

    def one(i, k, first=False):
        buf = state["buf"]
        dot(i, k, 1 - buf)
        finish_unit(*state["unit"], buf, first)
        state["buf"], state["unit"] = 1 - buf, (i, k)

    def run(i0, k0, width, start, count):
        buf = state["buf"]

        def unit(u):
            return i0 + u // width, k0 + u % width

        def body(it, carry):
            u = start + 2 * it
            dot(*unit(u), 1 - buf)
            finish_unit(carry[0], carry[1], buf)
            dot(*unit(u + 1), buf)
            finish_unit(*unit(u), 1 - buf)
            return unit(u + 1)

        last = tuple(jnp.int32(v) for v in state["unit"])
        state["unit"] = lax.fori_loop(0, count // 2, body, last)
        if count % 2:
            one(*unit(jnp.int32(start + count - 1)))

    rs[...] = jnp.zeros_like(rs)
    rl[...] = jnp.zeros_like(rl)
    cs[...] = jnp.zeros_like(cs)
    cl[...] = jnp.zeros_like(cl)
    for copy in own:
        copy.wait()
    save_txt(0)
    got_img(0)
    img.far(0)
    txt.far(0)
    img.second()
    txt.second()
    got_txt(4)
    txt.wait(("p0", 1), ("m0", 0))
    got_txt(3, 1)
    got_cross(0)
    dot(0, 0, 0)
    img.wait(("p0", 1), ("m0", 0))
    got_cross(4, 3, 1)
    one(0, 1, True)
    one(0, 2, True)
    run(0, 0, 4, 3, 13)
    got_img(4, 3, 1)
    for r in (txt, img):
        r.wait(("f0", 0), ("f0", 1))
    got_txt(2)
    run(4, 0, 4, 0, 4)
    got_cross(2)
    run(0, 4, 1, 0, 5)
    got_img(2)
    for r in (txt, img):
        r.far(1)
    txt.wait(("p1", 1), ("m1", 0))
    got_txt(7, 5)
    img.wait(("p1", 1), ("m1", 0))
    run(5, 0, 5, 0, 10)
    got_cross(7, 5)
    run(0, 5, 2, 0, 6)
    txt.wait(("f1", 0), ("f1", 1))
    got_txt(6)
    run(3, 5, 2, 0, 8)
    got_img(7, 5)
    img.wait(("f1", 0), ("f1", 1))
    got_cross(6)
    run(7, 0, 8, 0, 8)
    run(0, 7, 1, 0, 7)
    finish_unit(*state["unit"], state["buf"])

    for p in range(16):
        for q in range(n // 128):
            csum[2 * p + q:2 * p + q + 1, :] = jnp.sum(cs[p, :, q * 128:(q + 1) * 128], axis=0, keepdims=True)
    sums = []
    for dc, dy, dx in txt_offs:
        sums.append(net.send(csum, cbuf.at[dc * 8 + dy * 4 + (4 - dx) % 4], g.txt_peer(dc, dy, dx)))
    for i in range(8 * n // 128):
        rsum[i:i + 1, :] = jnp.sum(rs[i * 128:(i + 1) * 128, :].T, axis=0, keepdims=True)
    for dy, dz in img_offs:
        sums.append(net.send(rsum, rbuf.at[dy * 4 + (4 - dz) % 4], g.img_peer(dy, dz)))
    got_img(6)
    pos = jnp.sum(img_ref[...].astype(F32) * txt_ref[...].astype(F32), axis=1, keepdims=True) * scale
    rlsum = [jnp.sum(rl[i * 128:(i + 1) * 128, :].T, axis=0, keepdims=True) for i in range(8 * n // 128)]
    clsum = [jnp.sum(cl[p, :, q * 128:(q + 1) * 128], axis=0, keepdims=True) for p in range(16) for q in range(n // 128)]
    for copy in sums:
        copy.wait_recv()
    loss = jnp.zeros((2, 128), F32)
    dt = jnp.zeros((1, 128), F32)
    for dy, dz in [(0, 0)] + img_offs:
        k = 2 * POS[dy * 4 + dz]
        tot = rsum[k:k + 2, :]
        for oy, oz in img_offs:
            q = 2 * POS[(dy ^ oy) * 4 + (dz - oz) % 4]
            tot += rbuf[oy * 4 + oz, q:q + 2, :]
        a = 1.0 / tot
        a_ref[k:k + 2, :] = a * inv
        dt += a[0:1] * rlsum[k] + a[1:2] * rlsum[k + 1]
        if k == 0:
            loss += jnp.log(tot)
    for dc, dy, dx in [(0, 0, 0)] + txt_offs:
        k = 2 * (dc * 8 + POS[dy * 4 + dx])
        tot = csum[k:k + 2, :]
        for oc, oy, ox in txt_offs:
            q = 2 * ((dc ^ oc) * 8 + POS[(dy ^ oy) * 4 + (dx - ox) % 4])
            tot += cbuf[oc * 8 + oy * 4 + ox, q:q + 2, :]
        b = 1.0 / tot
        b_ref[k:k + 2, :] = b * inv
        dt += b[0:1] * clsum[k] + b[1:2] * clsum[k + 1]
        if k == 0:
            loss += jnp.log(tot)
    diag = jnp.sum(pos, axis=0, keepdims=True)
    first_lane = lax.broadcasted_iota(jnp.int32, (1, 128), 1) == 0
    diag = jnp.where(first_lane, 2.0 * diag, 0.0)
    part_ref[...] = jnp.zeros_like(part_ref)
    part_ref[0:1, :] = (jnp.sum(loss, axis=0, keepdims=True) - diag) * inv
    part_ref[1:2, :] = (dt - diag) * inv
    for buf in (0, 1):
        store(0, 0, buf).wait()
    for copy in saves:
        copy.wait()
    net.finish()


def forward(inv, scale, img, txt):
    n, d = img.shape
    vmem = pl.BlockSpec(memory_space=pltpu.VMEM)
    hbm = pl.BlockSpec(memory_space=pl.ANY)
    dma = pltpu.SemaphoreType.DMA
    return pl.pallas_call(
        functools.partial(forward_kernel, inv),
        out_shape=[jax.ShapeDtypeStruct((8, 2, 8, n, n), F32), jax.ShapeDtypeStruct((d, 8 * n), BF16),
                   jax.ShapeDtypeStruct((16 * n, d), BF16), jax.ShapeDtypeStruct((16, 128), F32),
                   jax.ShapeDtypeStruct((32, 128), F32), jax.ShapeDtypeStruct((8, 128), F32)],
        in_specs=[pl.BlockSpec(memory_space=pltpu.SMEM), vmem, vmem],
        out_specs=[hbm, hbm, hbm, vmem, vmem, vmem],
        scratch_shapes=[pltpu.VMEM((8, n, d), BF16), pltpu.VMEM((16, n, d), BF16), pltpu.VMEM((8, d, n), BF16),
                        pltpu.VMEM((2, n, n), F32), pltpu.VMEM((2, n, n), F32), pltpu.VMEM((2, n, n), F32),
                        pltpu.VMEM((2, n, n), F32), pltpu.VMEM((8 * n, 128), F32), pltpu.VMEM((8 * n, 128), F32),
                        pltpu.VMEM((16, 8, n), F32), pltpu.VMEM((16, 8, n), F32), pltpu.VMEM((16, 128), F32),
                        pltpu.VMEM((32, 128), F32), pltpu.VMEM((8, 16, 128), F32), pltpu.VMEM((16, 32, 128), F32),
                        dma((2,)), dma((16,)), dma((8,)), dma((2,)), dma((N_FORWARD,)), dma((N_FORWARD,))],
        compiler_params=pltpu.CompilerParams(collective_id=0, has_side_effects=True, vmem_limit_bytes=VMEM_LIMIT),
        name="forward_sums")(scale, img, txt)


ICUT = 144
TCUT = 432
ORDER = (6, 5, 7, 2, 1, 4, 3, 0)
KC = 512
N_REDUCE = 8 + 2 * (4 + 18 + 1) + 22


class Ring:
    def __init__(self, net, acc, buf, cut, plus, minus, pair):
        self.net, self.acc, self.buf = net, acc, buf
        self.cut, self.rows = cut, acc.shape[1]
        self.plus, self.minus, self.pair = plus, minus, pair
        self.early, self.streams = {}, {}

    def pair_send(self, d):
        at = pl.ds(self.cut, self.rows - self.cut)
        self.early[d] = self.net.send(self.acc.at[4 + d, at], self.buf.at[4 + d, at], self.pair)

    def pair_add(self, d):
        self.early[d].wait_recv()
        self.acc[d, self.cut:] += self.buf[4 + d, self.cut:]

    def where(self, name):
        if name == 2:
            return 0, self.cut, (self.rows - self.cut) // 2
        return 4 * name, 0, self.cut // 2

    def send(self, name, key, slot, half, to_slot, peer):
        _, lo, h = self.where(name)
        at = pl.ds(lo + half * h, h)
        self.streams[name, key] = self.net.send(self.acc.at[slot, at], self.buf.at[to_slot, at], peer)

    def far(self, name):
        b, _, _ = self.where(name)
        self.send(name, "a+", b + 2, 0, b + 2, self.plus)
        self.send(name, "a-", b + 2, 1, b + 2, self.minus)

    def plain_plus(self, name):
        b, _, _ = self.where(name)
        self.send(name, "b+1", b + 1, 1, b + 3, self.plus)

    def plain_minus(self, name):
        b, _, _ = self.where(name)
        self.send(name, "b-0", b + 3, 0, b + 1, self.minus)

    def mid(self, name):
        b, lo, h = self.where(name)
        self.streams[name, "a+"].wait_recv()
        self.acc[b + 1, lo:lo + h] += self.buf[b + 2, lo:lo + h]
        self.send(name, "b+0", b + 1, 0, b + 3, self.plus)
        self.streams[name, "a-"].wait_recv()
        self.acc[b + 3, lo + h:lo + 2 * h] += self.buf[b + 2, lo + h:lo + 2 * h]
        self.send(name, "b-1", b + 3, 1, b + 1, self.minus)

    def end(self, name):
        b, lo, h = self.where(name)
        for key in ("b+1", "b-0", "b+0", "b-1"):
            self.streams[name, key].wait_recv()
        self.acc[b, lo:lo + 2 * h] += self.buf[b + 1, lo:lo + 2 * h] + self.buf[b + 3, lo:lo + 2 * h]

    def pair_last(self):
        at = pl.ds(0, self.cut)
        self.late = self.net.send(self.acc.at[4, at], self.buf.at[0, at], self.pair)

    def pair_end(self):
        self.late.wait_recv()
        self.acc[0, 0:self.cut] += self.buf[0, 0:self.cut]

    def ready(self, step):
        if step == 0:
            self.pair_send(2)
            self.far(1)
        elif step == 1:
            self.pair_send(1)
            self.plain_plus(1)
        elif step == 2:
            self.pair_send(3)
            self.plain_minus(1)
            self.mid(1)
        elif step == 3:
            self.far(0)
            self.pair_add(2)
            self.far(2)
        elif step == 4:
            self.plain_plus(0)
            self.pair_add(1)
            self.plain_plus(2)
        elif step == 5:
            self.pair_send(0)
            self.end(1)
            self.pair_last()
        elif step == 6:
            self.plain_minus(0)
            self.pair_add(3)
            self.plain_minus(2)
            self.mid(0)

    def close(self):
        self.pair_add(0)
        self.end(0)
        self.pair_end()
        self.end(2)


def grads_kernel(inv, imgt_hbm, txt_hbm, e_hbm, a_ref, b_ref, part_ref, img_out, txt_out, part_out,
                 imgt, txt, erow, ecol, gb0, gb1, arow, stage, iacc, tacc, ibuf, tbuf, dbuf, pa, pb, psum,
                 local_sems, row_sems, col_sems, send_sems, recv_sems):
    g = Grid()
    n = iacc.shape[1]
    d = iacc.shape[2]
    m = imgt.shape[1]
    nt = txt.shape[0]
    img_offs = [(dy, dz) for dy in (0, 1) for dz in range(4) if (dy, dz) != (0, 0)]
    txt_offs = [(dc, dy, dx) for dc in (0, 1) for dy in (0, 1) for dx in range(4) if (dc, dy, dx) != (0, 0, 0)]

    def row_load(step):
        return pltpu.make_async_copy(e_hbm.at[POS[ORDER[step]]], erow.at[step % 2], row_sems.at[step % 2])

    def col_load(step, side):
        return pltpu.make_async_copy(e_hbm.at[:, side, POS[ORDER[step]]], ecol.at[side], col_sems.at[side])

    load_imgt = pltpu.make_async_copy(imgt_hbm, imgt, local_sems.at[0])
    load_txt = pltpu.make_async_copy(txt_hbm, txt, local_sems.at[1])
    cols = {}
    cols[0, 1] = col_load(0, 1)
    cols[0, 1].start()
    load_imgt.start()
    rows = {0: row_load(0)}
    rows[0].start()
    load_txt.start()
    cols[0, 0] = col_load(0, 0)
    cols[0, 0].start()
    for i in range(m // 128):
        arow[i * 128:(i + 1) * 128, :] = jnp.broadcast_to(a_ref[i:i + 1, :], (128, 128)).T
    greet([g.img_peer(*o) for o in img_offs] + [g.txt_peer(*o) for o in txt_offs])
    net = Net(send_sems, recv_sems)
    core = g.txt_peer(1, 0, 0)
    ia = g.z * 2 + g.y % 2
    ib = (g.x * 2 + g.y // 2) * 2 + g.c
    scal_a = [net.send(part_ref, pa.at[ia], g.img_peer(*o)) for o in img_offs]
    pa[ia] = part_ref[...]
    img = Ring(net, iacc, ibuf, ICUT, g.img_peer(0, 1), g.img_peer(0, 3), g.img_peer(1, 0))
    txr = Ring(net, tacc, tbuf, TCUT, g.txt_peer(0, 0, 1), g.txt_peer(0, 0, 3), g.txt_peer(0, 1, 0))

    def minus_diag(grad, q):
        r = lax.broadcasted_iota(jnp.int32, (n, 128), 0)
        c = lax.broadcasted_iota(jnp.int32, (n, 128), 1) + q * 128
        return grad - jnp.where(r == c, 2.0 * inv, 0.0)

    def col_slot(p, e_ref, out_ref):
        b = [b_ref[2 * p + q:2 * p + q + 1, :] for q in range(n // 128)]
        tiles = KC // n
        count = m // KC

        def grad(i, to, diag=False):
            for t in range(tiles):
                for q in range(n // 128):
                    lanes = slice(q * 128, (q + 1) * 128)
                    a = arow[pl.ds(pl.multiple_of(i * KC + t * n, n), n), :]
                    v = e_ref[i * tiles + t, :, lanes] * (a + b[q])
                    if diag and t == 0:
                        v = minus_diag(v, q)
                    to[t * n:(t + 1) * n, lanes] = v.astype(BF16)

        grad(0, gb0[0], diag=p == 0)
        out_ref[...] = jnp.zeros_like(out_ref)

        def body(it, carry):
            for half, (now, later) in enumerate(((gb0[0], gb0[1]), (gb0[1], gb0[0]))):
                i = 2 * it + half
                at = pl.ds(pl.multiple_of(i * KC, KC), KC)
                out_ref[...] += jnp.dot(imgt[:, at], now[...], preferred_element_type=F32)
                grad((i + 1) % count, later)
            return carry

        lax.fori_loop(0, count // 2, body, 0)

    def row_slot(p, e_ref, out_ref):
        tiles = KC // n
        count = nt // KC

        def grad(i, to, diag=False):
            for t in range(tiles):
                tile = i * tiles + t
                for q in range(n // 128):
                    lanes = slice(q * 128, (q + 1) * 128)
                    v = (e_ref[tile // 8, tile % 8, :, lanes]
                         * (arow[p * n:(p + 1) * n, :] + b_ref[pl.ds(2 * tile + q, 1), :]))
                    if diag and t == 0:
                        v = minus_diag(v, q)
                    to[:, t * n + q * 128:t * n + (q + 1) * 128] = v.astype(BF16)

        grad(0, gb1[0], diag=p == 0)
        out_ref[...] = jnp.zeros_like(out_ref)

        def body(it, carry):
            for half, (now, later) in enumerate(((gb1[0], gb1[1]), (gb1[1], gb1[0]))):
                i = 2 * it + half
                at = pl.ds(pl.multiple_of(i * KC, KC), KC)
                out_ref[...] += jnp.dot(now[...], txt[at, :], preferred_element_type=F32)
                grad((i + 1) % count, later)
            return carry

        lax.fori_loop(0, count // 2, body, 0)

    cross = {}
    for step, k in enumerate(ORDER):
        cols[step, 1].wait()
        if step == 0:
            load_imgt.wait()
        if step >= 2:
            cross[ORDER[step - 2]].wait_send()
        col_slot(8 + POS[k], ecol.at[1], stage.at[step % 2])
        cross[k] = net.send(stage.at[step % 2], dbuf.at[k], core)
        if step + 1 < len(ORDER):
            cols[step + 1, 1] = col_load(step + 1, 1)
            cols[step + 1, 1].start()
            rows[step + 1] = row_load(step + 1)
            rows[step + 1].start()
        rows[step].wait()
        if step == 0:
            load_txt.wait()
        row_slot(POS[k], erow.at[step % 2], iacc.at[k])
        img.ready(step)
        cols[step, 0].wait()
        col_slot(POS[k], ecol.at[0], tacc.at[k])
        if step + 1 < len(ORDER):
            cols[step + 1, 0] = col_load(step + 1, 0)
            cols[step + 1, 0].start()
        cross[k].wait_recv()
        tacc[k] += dbuf[k]
        txr.ready(step)
        if step == 1:
            for copy in scal_a:
                copy.wait_recv()
            total = pa[0]
            for q in range(1, 8):
                total += pa[q]
            psum[...] = total
            scal_b = [net.send(psum, pb.at[ib], g.txt_peer(*o)) for o in txt_offs]
            pb[ib] = total
    for r in (img, txr):
        r.mid(2)
    for copy in scal_b:
        copy.wait_recv()
    total = pb[0]
    for k in range(1, 16):
        total += pb[k]
    part_out[...] = total
    for r in (img, txr):
        r.close()
    img_out[...] = iacc[0]
    txt_out[...] = tacc[0]
    net.finish(skip=[cross[k] for k in ORDER[:-2]])


def grads(inv, imgt, txt_all, e, a, b, part):
    d, m = imgt.shape
    nt = txt_all.shape[0]
    n = m // 8
    vmem = pl.BlockSpec(memory_space=pltpu.VMEM)
    hbm = pl.BlockSpec(memory_space=pl.ANY)
    dma = pltpu.SemaphoreType.DMA
    return pl.pallas_call(
        functools.partial(grads_kernel, inv),
        out_shape=[jax.ShapeDtypeStruct((n, d), F32), jax.ShapeDtypeStruct((d, n), F32),
                   jax.ShapeDtypeStruct((8, 128), F32)],
        in_specs=[hbm, hbm, hbm, vmem, vmem, vmem],
        out_specs=[vmem] * 3,
        scratch_shapes=[pltpu.VMEM((d, m), BF16), pltpu.VMEM((nt, d), BF16), pltpu.VMEM((2, 2, 8, n, n), F32),
                        pltpu.VMEM((2, 8, n, n), F32), [pltpu.VMEM((KC, n), BF16)] * 2, [pltpu.VMEM((n, KC), BF16)] * 2,
                        pltpu.VMEM((m, 128), F32), pltpu.VMEM((2, d, n), F32), pltpu.VMEM((8, n, d), F32),
                        pltpu.VMEM((8, d, n), F32), pltpu.VMEM((8, n, d), F32), pltpu.VMEM((8, d, n), F32),
                        pltpu.VMEM((8, d, n), F32), pltpu.VMEM((8, 8, 128), F32), pltpu.VMEM((16, 8, 128), F32),
                        pltpu.VMEM((8, 128), F32), dma((2,)), dma((2,)), dma((2,)), dma((N_REDUCE,)),
                        dma((N_REDUCE,))],
        compiler_params=pltpu.CompilerParams(collective_id=2, has_side_effects=True, vmem_limit_bytes=VMEM_LIMIT),
        cost_estimate=pl.CostEstimate(flops=4 * m * nt * d, bytes_accessed=8 * m * nt, transcendentals=0),
        name="grads_reduce")(imgt, txt_all, e, a, b, part)


def solution(mesh):
    batch_spec = P(("row", "col"), None)
    shards = mesh.shape["row"] * mesh.shape["col"]

    def local_tile(img_loc, txt_loc, log_scale):
        n, d = img_loc.shape
        inv = 1.0 / (2 * n * shards)
        scale = jnp.exp(log_scale)
        e, imgt, txt_all, a, b, part = forward(inv, scale.reshape(1), img_loc, txt_loc)
        img_sum, txt_sum, tot = grads(inv, imgt, txt_all, e, a, b, part)
        d_img = (scale * img_sum).astype(BF16)
        d_txt = (scale * txt_sum).T.astype(BF16)
        tot = jnp.sum(tot[0:2], axis=1)
        return tot[0], d_img, d_txt, tot[1]

    return jax.shard_map(local_tile, mesh=mesh, in_specs=(batch_spec, batch_spec, P()),
                         out_specs=(P(), batch_spec, batch_spec, P()), check_vma=False)
```

time: 169 us -> 140 us (0.83)
  Pallas kernels: 154 us -> 133 us
  other arithmetic: 12.1 us -> 3.9 us
    pallas_call x3 -> x1, Pallas kernels: 89.1 us -> 69.3 us  [forward(): pl.pallas_call(functools.partial(forward_kernel, inv), out_shape=[jax.Sha...]
    reduce_sum x5 -> x0, other arithmetic: 7.58 us -> none  [the longest x2 4.33 us: local_tile(): rows = lambda v: jnp.sum(v, axis=1).reshape(-1, 128)]
where the time goes in v3:
time: 140 us; the launch traced here: 139 us
  Pallas kernels  133 us (95%)
  other arithmetic  3.9 us (3%)
  local copies, waits for them, and re-layouts  1.51 us (1%)
    pallas_call x1, Pallas kernels, forward(): pl.pallas_call(functools.partial(forward_kernel, inv), out_shape=[jax.Sha...  69.3 us
    pallas_call x1, Pallas kernels, grads(): pl.pallas_call(functools.partial(grads_kernel, inv), out_shape=[jax.Shape...  63.4 us

profile of v3, /device:TPU:1, one launch (start us, length us, event | category | flops | bytes accessed | tf_op | source)
XLA Modules:
  0.0 139.4 jit_solution(14159734459685754764)
XLA Ops:
  1.3 69.3 %forward_sums.1 = (f32[8,2,8,256,256]{4,3,2,1,0:T(8,128)}, bf16[768,2048]{1,0:T(8,128)(2,1)}, bf16[4096,768]{1,0:T(8,128)(2,1)}, f32[16,128]{1,0:T(8,128)}, f32[32,128]{1,0:T(8,128)}, /*index=5*/f32[8,128]{1,0:T(8,128)}) custom-call(f32[1]{0:T(128)} %bitcast.scale_ref, bf16[256,768]{1,0:T(8,128)(2,1)} %img_ref.1, bf16[256,768]{1,0:T(8,128)(2,1)} %txt_ref.1), custom_call_target="tpu_custom_call" | custom-call | tf_op jit(solution)/shard_map/forward_sums/pallas_call | solution.py:329
  70.6 63.4 %grads_reduce.1 = (f32[256,768]{1,0:T(8,128)}, f32[768,256]{1,0:T(8,128)}, f32[8,128]{1,0:T(8,128)}) custom-call(bf16[768,2048]{1,0:T(8,128)(2,1)} %get-tuple-element.13.imgt_hbm, bf16[4096,768]{1,0:T(8,128)(2,1)} %get-tuple-element.14.txt_hbm, f32[8,2,8,256,256]{4,3,2,1,0:T(8,128)} %get-tuple-element.15.e_hbm, f32[16,128]{1,0:T(8,128)} %get-tuple-element.16.a_ref, ...), custom_call_target="tpu_custom_call" | custom-call | flops 25769803776 | bytes 67108864 | tf_op jit(solution)/shard_map/grads_reduce/pallas_call | solution.py:609
  134.0 0.8 slice_reduce_fusion
  134.8 0.6 fusion.1
  135.4 1.9 %multiply_convert_fusion.1 = bf16[256,768]{1,0:T(8,128)(2,1)} fusion(f32[256,768]{1,0:T(8,128)} %get-tuple-element.20, f32[]{:T(128)} %exp.3), kind=kLoop, calls=%fused_computation.1 | loop fusion | flops 393216 | bytes 1179652 | tf_op jit(solution)/shard_map/convert_element_type | solution.py:637
  137.3 1.2 fusion
  138.5 0.9 copy.7

commit v4 on v3

--- a/solution.py
+++ b/solution.py
@@ -40,23 +40,39 @@
         return self.dev(self.z, y, (self.x + dx) % 4, c)
 
 
+def view(ref):
+    return ref[0].at[ref[1]] if isinstance(ref, tuple) else ref
+
+
+class Copy:
+    def __init__(self, net, i, src, dst, peer):
+        self.net, self.i, self.src, self.dst, self.peer = net, i, src, dst, peer
+
+    def make(self):
+        return pltpu.make_async_remote_copy(
+            src_ref=view(self.src), dst_ref=view(self.dst), send_sem=self.net.send_sems.at[self.i],
+            recv_sem=self.net.recv_sems.at[self.i], device_id=self.peer, device_id_type=MESH)
+
+    def wait_recv(self):
+        self.make().wait_recv()
+
+    def wait_send(self):
+        self.make().wait_send()
+
+
 class Net:
     def __init__(self, send_sems, recv_sems):
         self.send_sems, self.recv_sems, self.copies = send_sems, recv_sems, []
 
     def send(self, src, dst, peer):
-        i = len(self.copies)
-        copy = pltpu.make_async_remote_copy(
-            src_ref=src, dst_ref=dst, send_sem=self.send_sems.at[i], recv_sem=self.recv_sems.at[i],
-            device_id=peer, device_id_type=MESH)
-        copy.start()
+        copy = Copy(self, len(self.copies), src, dst, peer)
+        copy.make().start()
         self.copies.append(copy)
         return copy
 
-    def finish(self, skip=()):
+    def finish(self):
         for copy in self.copies:
-            if not any(copy is other for other in skip):
-                copy.wait_send()
+            copy.wait_send()
 
 
 def greet(peers):
@@ -71,7 +87,8 @@
             g.txt_peer(0, 1, 0), g.txt_peer(1, 0, 0)]
 
 
-POS = {0: 0, 4: 1, 3: 2, 1: 3, 2: 4, 7: 5, 5: 6, 6: 7}
+POS = {0: 0, 3: 1, 4: 2, 1: 3, 2: 4, 7: 5, 5: 6, 6: 7}
+DEEP = 4
 N_FORWARD = 2 * 18 + 9 + 22
 
 
@@ -168,13 +185,20 @@
             dots[buf][side] = lax.dot_general(lhs, txt_all[8 * side + k], (((1,), (1,)), ((), ())),
                                               preferred_element_type=F32)
 
-    def store(i, k, buf):
-        return pltpu.make_async_copy(stage[buf], e_out.at[i, :, k], e_sems.at[buf])
-
-    def finish_unit(i, k, buf, first=False):
-        if not first:
-            store(i, k, buf).wait()
-        at = pl.ds(i * n, n) if isinstance(i, int) else pl.ds(pl.multiple_of(i * n, n), n)
+    def store(i, k, buf, slot):
+        return pltpu.make_async_copy(stage[buf].at[slot], e_out.at[i, :, k], e_sems.at[buf * DEEP + slot])
+
+    def free(buf, use):
+        if isinstance(use, int):
+            if use >= DEEP:
+                store(0, 0, buf, use % DEEP).wait()
+        else:
+            @pl.when(use >= DEEP)
+            def _():
+                store(0, 0, buf, use % DEEP).wait()
+
+    def finish_unit(i, k, buf, use):
+        slot = use % DEEP
         for blk in range(n // 32):
             lo = blk * 32
             rows = pl.ds(i * n + lo, 32) if isinstance(i, int) else pl.ds(pl.multiple_of(i * n + lo, 32), 32)
@@ -183,7 +207,7 @@
                 logits = scale * dots[buf][side, lo:lo + 32, :]
                 e = jnp.exp(logits)
                 el = e * logits
-                stage[buf][side, lo:lo + 32, :] = e
+                stage[buf][slot, side, lo:lo + 32, :] = e
                 for q in range(n // 128):
                     racc += e[:, q * 128:(q + 1) * 128]
                     lacc += el[:, q * 128:(q + 1) * 128]
@@ -191,32 +215,44 @@
                 cl[8 * side + k] += jnp.sum(el.reshape(4, 8, n), axis=0)
             rs[rows, :] = racc
             rl[rows, :] = lacc
-        store(i, k, buf).start()
-
-    state = {"buf": 0, "unit": (0, 0)}
-
-    def one(i, k, first=False):
+        store(i, k, buf, slot).start()
+
+    state = {"buf": 0, "unit": (0, 0), "uses": [0, 0]}
+
+    def last_unit():
         buf = state["buf"]
+        free(buf, state["uses"][buf])
+        finish_unit(*state["unit"], buf, state["uses"][buf])
+        state["uses"][buf] += 1
+
+    def one(i, k):
+        buf = state["buf"]
+        free(buf, state["uses"][buf])
         dot(i, k, 1 - buf)
-        finish_unit(*state["unit"], buf, first)
+        finish_unit(*state["unit"], buf, state["uses"][buf])
+        state["uses"][buf] += 1
         state["buf"], state["unit"] = 1 - buf, (i, k)
 
     def run(i0, k0, width, start, count):
         buf = state["buf"]
+        uses = list(state["uses"])
 
         def unit(u):
             return i0 + u // width, k0 + u % width
 
         def body(it, carry):
             u = start + 2 * it
+            free(buf, uses[buf] + it)
+            free(1 - buf, uses[1 - buf] + it)
             dot(*unit(u), 1 - buf)
-            finish_unit(carry[0], carry[1], buf)
+            finish_unit(carry[0], carry[1], buf, uses[buf] + it)
             dot(*unit(u + 1), buf)
-            finish_unit(*unit(u), 1 - buf)
+            finish_unit(*unit(u), 1 - buf, uses[1 - buf] + it)
             return unit(u + 1)
 
         last = tuple(jnp.int32(v) for v in state["unit"])
         state["unit"] = lax.fori_loop(0, count // 2, body, last)
+        state["uses"] = [v + count // 2 for v in uses]
         if count % 2:
             one(*unit(jnp.int32(start + count - 1)))
 
@@ -239,9 +275,7 @@
     dot(0, 0, 0)
     img.wait(("p0", 1), ("m0", 0))
     got_cross(4, 3, 1)
-    one(0, 1, True)
-    one(0, 2, True)
-    run(0, 0, 4, 3, 13)
+    run(0, 0, 4, 1, 15)
     got_img(4, 3, 1)
     for r in (txt, img):
         r.wait(("f0", 0), ("f0", 1))
@@ -266,7 +300,7 @@
     got_cross(6)
     run(7, 0, 8, 0, 8)
     run(0, 7, 1, 0, 7)
-    finish_unit(*state["unit"], state["buf"])
+    last_unit()
 
     for p in range(16):
         for q in range(n // 128):
@@ -315,7 +349,8 @@
     part_ref[0:1, :] = (jnp.sum(loss, axis=0, keepdims=True) - diag) * inv
     part_ref[1:2, :] = (dt - diag) * inv
     for buf in (0, 1):
-        store(0, 0, buf).wait()
+        for slot in range(DEEP):
+            store(0, 0, buf, slot).wait()
     for copy in saves:
         copy.wait()
     net.finish()
@@ -334,11 +369,11 @@
         in_specs=[pl.BlockSpec(memory_space=pltpu.SMEM), vmem, vmem],
         out_specs=[hbm, hbm, hbm, vmem, vmem, vmem],
         scratch_shapes=[pltpu.VMEM((8, n, d), BF16), pltpu.VMEM((16, n, d), BF16), pltpu.VMEM((8, d, n), BF16),
-                        pltpu.VMEM((2, n, n), F32), pltpu.VMEM((2, n, n), F32), pltpu.VMEM((2, n, n), F32),
-                        pltpu.VMEM((2, n, n), F32), pltpu.VMEM((8 * n, 128), F32), pltpu.VMEM((8 * n, 128), F32),
+                        pltpu.VMEM((2, n, n), F32), pltpu.VMEM((2, n, n), F32), pltpu.VMEM((DEEP, 2, n, n), F32),
+                        pltpu.VMEM((DEEP, 2, n, n), F32), pltpu.VMEM((8 * n, 128), F32), pltpu.VMEM((8 * n, 128), F32),
                         pltpu.VMEM((16, 8, n), F32), pltpu.VMEM((16, 8, n), F32), pltpu.VMEM((16, 128), F32),
                         pltpu.VMEM((32, 128), F32), pltpu.VMEM((8, 16, 128), F32), pltpu.VMEM((16, 32, 128), F32),
-                        dma((2,)), dma((16,)), dma((8,)), dma((2,)), dma((N_FORWARD,)), dma((N_FORWARD,))],
+                        dma((2 * DEEP,)), dma((16,)), dma((8,)), dma((2,)), dma((N_FORWARD,)), dma((N_FORWARD,))],
         compiler_params=pltpu.CompilerParams(collective_id=0, has_side_effects=True, vmem_limit_bytes=VMEM_LIMIT),
         name="forward_sums")(scale, img, txt)
 
@@ -346,8 +381,7 @@
 ICUT = 144
 TCUT = 432
 ORDER = (6, 5, 7, 2, 1, 4, 3, 0)
-KC = 512
-N_REDUCE = 8 + 2 * (4 + 18 + 1) + 22
+N_REDUCE = 2 * (4 + 18 + 1) + 22
 
 
 class Ring:
@@ -359,11 +393,11 @@
 
     def pair_send(self, d):
         at = pl.ds(self.cut, self.rows - self.cut)
-        self.early[d] = self.net.send(self.acc.at[4 + d, at], self.buf.at[4 + d, at], self.pair)
+        self.early[d] = self.net.send((self.acc, (POS[4 + d], at)), (self.buf, (4 + d, at)), self.pair)
 
     def pair_add(self, d):
         self.early[d].wait_recv()
-        self.acc[d, self.cut:] += self.buf[4 + d, self.cut:]
+        self.acc[POS[d], self.cut:] += self.buf[4 + d, self.cut:]
 
     def where(self, name):
         if name == 2:
@@ -373,7 +407,7 @@
     def send(self, name, key, slot, half, to_slot, peer):
         _, lo, h = self.where(name)
         at = pl.ds(lo + half * h, h)
-        self.streams[name, key] = self.net.send(self.acc.at[slot, at], self.buf.at[to_slot, at], peer)
+        self.streams[name, key] = self.net.send((self.acc, (POS[slot], at)), (self.buf, (to_slot, at)), peer)
 
     def far(self, name):
         b, _, _ = self.where(name)
@@ -391,21 +425,21 @@
     def mid(self, name):
         b, lo, h = self.where(name)
         self.streams[name, "a+"].wait_recv()
-        self.acc[b + 1, lo:lo + h] += self.buf[b + 2, lo:lo + h]
+        self.acc[POS[b + 1], lo:lo + h] += self.buf[b + 2, lo:lo + h]
         self.send(name, "b+0", b + 1, 0, b + 3, self.plus)
         self.streams[name, "a-"].wait_recv()
-        self.acc[b + 3, lo + h:lo + 2 * h] += self.buf[b + 2, lo + h:lo + 2 * h]
+        self.acc[POS[b + 3], lo + h:lo + 2 * h] += self.buf[b + 2, lo + h:lo + 2 * h]
         self.send(name, "b-1", b + 3, 1, b + 1, self.minus)
 
     def end(self, name):
         b, lo, h = self.where(name)
         for key in ("b+1", "b-0", "b+0", "b-1"):
             self.streams[name, key].wait_recv()
-        self.acc[b, lo:lo + 2 * h] += self.buf[b + 1, lo:lo + 2 * h] + self.buf[b + 3, lo:lo + 2 * h]
+        self.acc[POS[b], lo:lo + 2 * h] += self.buf[b + 1, lo:lo + 2 * h] + self.buf[b + 3, lo:lo + 2 * h]
 
     def pair_last(self):
         at = pl.ds(0, self.cut)
-        self.late = self.net.send(self.acc.at[4, at], self.buf.at[0, at], self.pair)
+        self.late = self.net.send((self.acc, (POS[4], at)), (self.buf, (0, at)), self.pair)
 
     def pair_end(self):
         self.late.wait_recv()
@@ -448,142 +482,129 @@
 
 
 def grads_kernel(inv, imgt_hbm, txt_hbm, e_hbm, a_ref, b_ref, part_ref, img_out, txt_out, part_out,
-                 imgt, txt, erow, ecol, gb0, gb1, arow, stage, iacc, tacc, ibuf, tbuf, dbuf, pa, pb, psum,
-                 local_sems, row_sems, col_sems, send_sems, recv_sems):
+                 imgt, txt, erow, ecol, gb_row, gb_near, gb_far, arow, stage, iacc, tacc, ibuf, tbuf, dbuf, pa, pb,
+                 psum, local_sems, e_sems, send_sems, recv_sems, cross_send, cross_recv):
     g = Grid()
     n = iacc.shape[1]
-    d = iacc.shape[2]
     m = imgt.shape[1]
-    nt = txt.shape[0]
     img_offs = [(dy, dz) for dy in (0, 1) for dz in range(4) if (dy, dz) != (0, 0)]
     txt_offs = [(dc, dy, dx) for dc in (0, 1) for dy in (0, 1) for dx in range(4) if (dc, dy, dx) != (0, 0, 0)]
-
-    def row_load(step):
-        return pltpu.make_async_copy(e_hbm.at[POS[ORDER[step]]], erow.at[step % 2], row_sems.at[step % 2])
-
-    def col_load(step, side):
-        return pltpu.make_async_copy(e_hbm.at[:, side, POS[ORDER[step]]], ecol.at[side], col_sems.at[side])
+    last = len(ORDER) - 1
+
+    def row_load(p):
+        return pltpu.make_async_copy(e_hbm.at[p], erow, e_sems.at[2])
+
+    def col_load(p, side):
+        return pltpu.make_async_copy(e_hbm.at[:, side, p], ecol.at[side], e_sems.at[side])
 
     load_imgt = pltpu.make_async_copy(imgt_hbm, imgt, local_sems.at[0])
     load_txt = pltpu.make_async_copy(txt_hbm, txt, local_sems.at[1])
-    cols = {}
-    cols[0, 1] = col_load(0, 1)
-    cols[0, 1].start()
+    col_load(last, 1).start()
     load_imgt.start()
-    rows = {0: row_load(0)}
-    rows[0].start()
+    row_load(last).start()
     load_txt.start()
-    cols[0, 0] = col_load(0, 0)
-    cols[0, 0].start()
+    col_load(last, 0).start()
     for i in range(m // 128):
         arow[i * 128:(i + 1) * 128, :] = jnp.broadcast_to(a_ref[i:i + 1, :], (128, 128)).T
     greet([g.img_peer(*o) for o in img_offs] + [g.txt_peer(*o) for o in txt_offs])
     net = Net(send_sems, recv_sems)
     core = g.txt_peer(1, 0, 0)
+    img_peers = [g.img_peer(*o) for o in img_offs]
+    txt_peers = [g.txt_peer(*o) for o in txt_offs]
     ia = g.z * 2 + g.y % 2
     ib = (g.x * 2 + g.y // 2) * 2 + g.c
-    scal_a = [net.send(part_ref, pa.at[ia], g.img_peer(*o)) for o in img_offs]
+    scal_a = [net.send(part_ref, (pa, ia), peer) for peer in img_peers]
+    scal_b = []
     pa[ia] = part_ref[...]
     img = Ring(net, iacc, ibuf, ICUT, g.img_peer(0, 1), g.img_peer(0, 3), g.img_peer(1, 0))
     txr = Ring(net, tacc, tbuf, TCUT, g.txt_peer(0, 0, 1), g.txt_peer(0, 0, 3), g.txt_peer(0, 1, 0))
 
-    def minus_diag(grad, q):
+    def minus_diag(grad, q, p):
         r = lax.broadcasted_iota(jnp.int32, (n, 128), 0)
         c = lax.broadcasted_iota(jnp.int32, (n, 128), 1) + q * 128
-        return grad - jnp.where(r == c, 2.0 * inv, 0.0)
-
-    def col_slot(p, e_ref, out_ref):
-        b = [b_ref[2 * p + q:2 * p + q + 1, :] for q in range(n // 128)]
-        tiles = KC // n
-        count = m // KC
-
-        def grad(i, to, diag=False):
-            for t in range(tiles):
-                for q in range(n // 128):
-                    lanes = slice(q * 128, (q + 1) * 128)
-                    a = arow[pl.ds(pl.multiple_of(i * KC + t * n, n), n), :]
-                    v = e_ref[i * tiles + t, :, lanes] * (a + b[q])
-                    if diag and t == 0:
-                        v = minus_diag(v, q)
-                    to[t * n:(t + 1) * n, lanes] = v.astype(BF16)
-
-        grad(0, gb0[0], diag=p == 0)
-        out_ref[...] = jnp.zeros_like(out_ref)
-
-        def body(it, carry):
-            for half, (now, later) in enumerate(((gb0[0], gb0[1]), (gb0[1], gb0[0]))):
-                i = 2 * it + half
-                at = pl.ds(pl.multiple_of(i * KC, KC), KC)
-                out_ref[...] += jnp.dot(imgt[:, at], now[...], preferred_element_type=F32)
-                grad((i + 1) % count, later)
-            return carry
-
-        lax.fori_loop(0, count // 2, body, 0)
-
-    def row_slot(p, e_ref, out_ref):
-        tiles = KC // n
-        count = nt // KC
-
-        def grad(i, to, diag=False):
-            for t in range(tiles):
-                tile = i * tiles + t
-                for q in range(n // 128):
-                    lanes = slice(q * 128, (q + 1) * 128)
-                    v = (e_ref[tile // 8, tile % 8, :, lanes]
-                         * (arow[p * n:(p + 1) * n, :] + b_ref[pl.ds(2 * tile + q, 1), :]))
-                    if diag and t == 0:
-                        v = minus_diag(v, q)
-                    to[:, t * n + q * 128:t * n + (q + 1) * 128] = v.astype(BF16)
-
-        grad(0, gb1[0], diag=p == 0)
-        out_ref[...] = jnp.zeros_like(out_ref)
-
-        def body(it, carry):
-            for half, (now, later) in enumerate(((gb1[0], gb1[1]), (gb1[1], gb1[0]))):
-                i = 2 * it + half
-                at = pl.ds(pl.multiple_of(i * KC, KC), KC)
-                out_ref[...] += jnp.dot(now[...], txt[at, :], preferred_element_type=F32)
-                grad((i + 1) % count, later)
-            return carry
-
-        lax.fori_loop(0, count // 2, body, 0)
-
-    cross = {}
-    for step, k in enumerate(ORDER):
-        cols[step, 1].wait()
-        if step == 0:
-            load_imgt.wait()
-        if step >= 2:
-            cross[ORDER[step - 2]].wait_send()
-        col_slot(8 + POS[k], ecol.at[1], stage.at[step % 2])
-        cross[k] = net.send(stage.at[step % 2], dbuf.at[k], core)
-        if step + 1 < len(ORDER):
-            cols[step + 1, 1] = col_load(step + 1, 1)
-            cols[step + 1, 1].start()
-            rows[step + 1] = row_load(step + 1)
-            rows[step + 1].start()
-        rows[step].wait()
-        if step == 0:
-            load_txt.wait()
-        row_slot(POS[k], erow.at[step % 2], iacc.at[k])
-        img.ready(step)
-        cols[step, 0].wait()
-        col_slot(POS[k], ecol.at[0], tacc.at[k])
-        if step + 1 < len(ORDER):
-            cols[step + 1, 0] = col_load(step + 1, 0)
-            cols[step + 1, 0].start()
-        cross[k].wait_recv()
-        tacc[k] += dbuf[k]
-        txr.ready(step)
-        if step == 1:
-            for copy in scal_a:
-                copy.wait_recv()
-            total = pa[0]
-            for q in range(1, 8):
-                total += pa[q]
-            psum[...] = total
-            scal_b = [net.send(psum, pb.at[ib], g.txt_peer(*o)) for o in txt_offs]
-            pb[ib] = total
+        return grad - jnp.where(r == c, jnp.where(p == 0, 2.0 * inv, 0.0), 0.0)
+
+    def col_grad(p, side, to):
+        for t in range(m // n):
+            a = arow[t * n:(t + 1) * n, :]
+            for q in range(n // 128):
+                lanes = slice(q * 128, (q + 1) * 128)
+                v = ecol[side, t, :, lanes] * (a + b_ref[pl.ds(2 * (p + 8 * side) + q, 1), :])
+                if side == 0 and t == 0:
+                    v = minus_diag(v, q, p)
+                to[t * n:(t + 1) * n, lanes] = v.astype(BF16)
+
+    def row_grad(p):
+        a = arow[pl.ds(pl.multiple_of(p * n, n), n), :]
+        for t in range(16):
+            for q in range(n // 128):
+                lanes = slice(q * 128, (q + 1) * 128)
+                v = erow[t // 8, t % 8, :, lanes] * (a + b_ref[2 * t + q:2 * t + q + 1, :])
+                if t == 0:
+                    v = minus_diag(v, q, p)
+                gb_row[:, t * n + q * 128:t * n + (q + 1) * 128] = v.astype(BF16)
+
+    def crossing(s):
+        return pltpu.make_async_remote_copy(
+            src_ref=stage.at[s % 2], dst_ref=dbuf.at[last - s], send_sem=cross_send.at[s], recv_sem=cross_recv.at[s],
+            device_id=core, device_id_type=MESH)
+
+    col_load(last, 1).wait()
+    col_grad(last, 1, gb_far)
+    load_imgt.wait()
+    load_txt.wait()
+
+    def step(s, carry):
+        p = last - s
+        row_load(p).wait()
+
+        @pl.when(s >= 2)
+        def _():
+            crossing(s - 2).wait_send()
+
+        stage[s % 2] = jnp.dot(imgt[...], gb_far[...], preferred_element_type=F32)
+        row_grad(p)
+        crossing(s).start()
+
+        @pl.when(s < last)
+        def _():
+            row_load(p - 1).start()
+            col_load(p - 1, 1).start()
+
+        col_load(p, 0).wait()
+        iacc[p] = jnp.dot(gb_row[...], txt[...], preferred_element_type=F32)
+        col_grad(p, 0, gb_near)
+
+        @pl.when(s < last)
+        def _():
+            col_load(p - 1, 0).start()
+            col_load(p - 1, 1).wait()
+
+        for i in range(last + 1):
+            @pl.when(s == i)
+            def _():
+                img.ready(i)
+
+        tacc[p] = jnp.dot(imgt[...], gb_near[...], preferred_element_type=F32)
+        col_grad(p - 1 + (s // last), 1, gb_far)
+        crossing(s).wait_recv()
+        tacc[p] += dbuf[p]
+        for i in range(last + 1):
+            @pl.when(s == i)
+            def _():
+                txr.ready(i)
+                if i == 1:
+                    for copy in scal_a:
+                        copy.wait_recv()
+                    total = pa[0]
+                    for q in range(1, 8):
+                        total += pa[q]
+                    psum[...] = total
+                    scal_b.extend(net.send(psum, (pb, ib), peer) for peer in txt_peers)
+                    pb[ib] = total
+        return carry
+
+    lax.fori_loop(0, last + 1, step, 0)
     for r in (img, txr):
         r.mid(2)
     for copy in scal_b:
@@ -596,7 +617,9 @@
         r.close()
     img_out[...] = iacc[0]
     txt_out[...] = tacc[0]
-    net.finish(skip=[cross[k] for k in ORDER[:-2]])
+    crossing(last - 1).wait_send()
+    crossing(last).wait_send()
+    net.finish()
 
 
 def grads(inv, imgt, txt_all, e, a, b, part):
@@ -612,13 +635,13 @@
                    jax.ShapeDtypeStruct((8, 128), F32)],
         in_specs=[hbm, hbm, hbm, vmem, vmem, vmem],
         out_specs=[vmem] * 3,
-        scratch_shapes=[pltpu.VMEM((d, m), BF16), pltpu.VMEM((nt, d), BF16), pltpu.VMEM((2, 2, 8, n, n), F32),
-                        pltpu.VMEM((2, 8, n, n), F32), [pltpu.VMEM((KC, n), BF16)] * 2, [pltpu.VMEM((n, KC), BF16)] * 2,
-                        pltpu.VMEM((m, 128), F32), pltpu.VMEM((2, d, n), F32), pltpu.VMEM((8, n, d), F32),
-                        pltpu.VMEM((8, d, n), F32), pltpu.VMEM((8, n, d), F32), pltpu.VMEM((8, d, n), F32),
-                        pltpu.VMEM((8, d, n), F32), pltpu.VMEM((8, 8, 128), F32), pltpu.VMEM((16, 8, 128), F32),
-                        pltpu.VMEM((8, 128), F32), dma((2,)), dma((2,)), dma((2,)), dma((N_REDUCE,)),
-                        dma((N_REDUCE,))],
+        scratch_shapes=[pltpu.VMEM((d, m), BF16), pltpu.VMEM((nt, d), BF16), pltpu.VMEM((2, 8, n, n), F32),
+                        pltpu.VMEM((2, 8, n, n), F32), pltpu.VMEM((n, nt), BF16), pltpu.VMEM((m, n), BF16),
+                        pltpu.VMEM((m, n), BF16), pltpu.VMEM((m, 128), F32), pltpu.VMEM((2, d, n), F32),
+                        pltpu.VMEM((8, n, d), F32), pltpu.VMEM((8, d, n), F32), pltpu.VMEM((8, n, d), F32),
+                        pltpu.VMEM((8, d, n), F32), pltpu.VMEM((8, d, n), F32), pltpu.VMEM((8, 8, 128), F32),
+                        pltpu.VMEM((16, 8, 128), F32), pltpu.VMEM((8, 128), F32), dma((2,)), dma((3,)),
+                        dma((N_REDUCE,)), dma((N_REDUCE,)), dma((8,)), dma((8,))],
         compiler_params=pltpu.CompilerParams(collective_id=2, has_side_effects=True, vmem_limit_bytes=VMEM_LIMIT),
         cost_estimate=pl.CostEstimate(flops=4 * m * nt * d, bytes_accessed=8 * m * nt, transcendentals=0),
         name="grads_reduce")(imgt, txt_all, e, a, b, part)

time: 140 us -> 140 us (level)
    pallas_call x1, Pallas kernels: 63.4 us -> 77.3 us  [grads(): pl.pallas_call(functools.partial(grads_kernel, inv), out_shape=[jax.Shape...]
    pallas_call x1, Pallas kernels: 69.3 us -> 55.4 us  [forward(): pl.pallas_call(functools.partial(forward_kernel, inv), out_shape=[jax.Sha...]
where the time goes in v4:
time: 140 us; the launch traced here: 139 us
  Pallas kernels  133 us (95%)
  other arithmetic  3.9 us (3%)
  local copies, waits for them, and re-layouts  1.51 us (1%)
    pallas_call x1, Pallas kernels, grads(): pl.pallas_call(functools.partial(grads_kernel, inv), out_shape=[jax.Shape...  77.3 us
    pallas_call x1, Pallas kernels, forward(): pl.pallas_call(functools.partial(forward_kernel, inv), out_shape=[jax.Sha...  55.4 us

profile of v4, /device:TPU:1, one launch (start us, length us, event | category | flops | bytes accessed | tf_op | source)
XLA Modules:
  0.0 139.5 jit_solution(8166433922896065275)
XLA Ops:
  1.3 55.4 %forward_sums.1 = (f32[8,2,8,256,256]{4,3,2,1,0:T(8,128)}, bf16[768,2048]{1,0:T(8,128)(2,1)}, bf16[4096,768]{1,0:T(8,128)(2,1)}, f32[16,128]{1,0:T(8,128)}, f32[32,128]{1,0:T(8,128)}, /*index=5*/f32[8,128]{1,0:T(8,128)}) custom-call(f32[1]{0:T(128)} %bitcast.scale_ref, bf16[256,768]{1,0:T(8,128)(2,1)} %img_ref.1, bf16[256,768]{1,0:T(8,128)(2,1)} %txt_ref.1), custom_call_target="tpu_custom_call" | custom-call | tf_op jit(solution)/shard_map/forward_sums/pallas_call | solution.py:364
  56.7 77.3 %grads_reduce.1 = (f32[256,768]{1,0:T(8,128)}, f32[768,256]{1,0:T(8,128)}, f32[8,128]{1,0:T(8,128)}) custom-call(bf16[768,2048]{1,0:T(8,128)(2,1)} %get-tuple-element.13.imgt_hbm, bf16[4096,768]{1,0:T(8,128)(2,1)} %get-tuple-element.14.txt_hbm, f32[8,2,8,256,256]{4,3,2,1,0:T(8,128)} %get-tuple-element.15.e_hbm, f32[16,128]{1,0:T(8,128)} %get-tuple-element.16.a_ref, ...), custom_call_target="tpu_custom_call" | custom-call | flops 25769803776 | bytes 67108864 | tf_op jit(solution)/shard_map/grads_reduce/pallas_call | solution.py:632
  134.0 0.8 slice_reduce_fusion
  134.8 0.6 fusion.1
  135.4 1.9 %multiply_convert_fusion.1 = bf16[256,768]{1,0:T(8,128)(2,1)} fusion(f32[256,768]{1,0:T(8,128)} %get-tuple-element.20, f32[]{:T(128)} %exp.3), kind=kLoop, calls=%fused_computation.1 | loop fusion | flops 393216 | bytes 1179652 | tf_op jit(solution)/shard_map/convert_element_type | solution.py:660
  137.3 1.2 fusion
  138.5 0.9 copy.7

commit v5 on v3

--- a/solution.py
+++ b/solution.py
@@ -10,7 +10,7 @@
 MESH = pl.DeviceIdType.MESH
 F32 = jnp.float32
 BF16 = jnp.bfloat16
-VMEM_LIMIT = 64_000_000
+VMEM_LIMIT = 67_043_328
 
 
 class Grid:
@@ -40,16 +40,33 @@
         return self.dev(self.z, y, (self.x + dx) % 4, c)
 
 
+def view(ref):
+    return ref[0].at[ref[1]] if isinstance(ref, tuple) else ref
+
+
+class Copy:
+    def __init__(self, net, i, src, dst, peer):
+        self.net, self.i, self.src, self.dst, self.peer = net, i, src, dst, peer
+
+    def make(self):
+        return pltpu.make_async_remote_copy(
+            src_ref=view(self.src), dst_ref=view(self.dst), send_sem=self.net.send_sems.at[self.i],
+            recv_sem=self.net.recv_sems.at[self.i], device_id=self.peer, device_id_type=MESH)
+
+    def wait_recv(self):
+        self.make().wait_recv()
+
+    def wait_send(self):
+        self.make().wait_send()
+
+
 class Net:
     def __init__(self, send_sems, recv_sems):
         self.send_sems, self.recv_sems, self.copies = send_sems, recv_sems, []
 
     def send(self, src, dst, peer):
-        i = len(self.copies)
-        copy = pltpu.make_async_remote_copy(
-            src_ref=src, dst_ref=dst, send_sem=self.send_sems.at[i], recv_sem=self.recv_sems.at[i],
-            device_id=peer, device_id_type=MESH)
-        copy.start()
+        copy = Copy(self, len(self.copies), src, dst, peer)
+        copy.make().start()
         self.copies.append(copy)
         return copy
 
@@ -71,7 +88,8 @@
             g.txt_peer(0, 1, 0), g.txt_peer(1, 0, 0)]
 
 
-POS = {0: 0, 4: 1, 3: 2, 1: 3, 2: 4, 7: 5, 5: 6, 6: 7}
+POS = {0: 0, 3: 1, 4: 2, 1: 3, 2: 4, 7: 5, 5: 6, 6: 7}
+DEEP = 4
 N_FORWARD = 2 * 18 + 9 + 22
 
 
@@ -168,13 +186,20 @@
             dots[buf][side] = lax.dot_general(lhs, txt_all[8 * side + k], (((1,), (1,)), ((), ())),
                                               preferred_element_type=F32)
 
-    def store(i, k, buf):
-        return pltpu.make_async_copy(stage[buf], e_out.at[i, :, k], e_sems.at[buf])
-
-    def finish_unit(i, k, buf, first=False):
-        if not first:
-            store(i, k, buf).wait()
-        at = pl.ds(i * n, n) if isinstance(i, int) else pl.ds(pl.multiple_of(i * n, n), n)
+    def store(i, k, buf, slot):
+        return pltpu.make_async_copy(stage[buf].at[slot], e_out.at[i, :, k], e_sems.at[buf * DEEP + slot])
+
+    def free(buf, use):
+        if isinstance(use, int):
+            if use >= DEEP:
+                store(0, 0, buf, use % DEEP).wait()
+        else:
+            @pl.when(use >= DEEP)
+            def _():
+                store(0, 0, buf, use % DEEP).wait()
+
+    def finish_unit(i, k, buf, use):
+        slot = use % DEEP
         for blk in range(n // 32):
             lo = blk * 32
             rows = pl.ds(i * n + lo, 32) if isinstance(i, int) else pl.ds(pl.multiple_of(i * n + lo, 32), 32)
@@ -183,7 +208,7 @@
                 logits = scale * dots[buf][side, lo:lo + 32, :]
                 e = jnp.exp(logits)
                 el = e * logits
-                stage[buf][side, lo:lo + 32, :] = e
+                stage[buf][slot, side, lo:lo + 32, :] = e
                 for q in range(n // 128):
                     racc += e[:, q * 128:(q + 1) * 128]
                     lacc += el[:, q * 128:(q + 1) * 128]
@@ -191,32 +216,44 @@
                 cl[8 * side + k] += jnp.sum(el.reshape(4, 8, n), axis=0)
             rs[rows, :] = racc
             rl[rows, :] = lacc
-        store(i, k, buf).start()
-
-    state = {"buf": 0, "unit": (0, 0)}
-
-    def one(i, k, first=False):
+        store(i, k, buf, slot).start()
+
+    state = {"buf": 0, "unit": (0, 0), "uses": [0, 0]}
+
+    def last_unit():
         buf = state["buf"]
+        free(buf, state["uses"][buf])
+        finish_unit(*state["unit"], buf, state["uses"][buf])
+        state["uses"][buf] += 1
+
+    def one(i, k):
+        buf = state["buf"]
+        free(buf, state["uses"][buf])
         dot(i, k, 1 - buf)
-        finish_unit(*state["unit"], buf, first)
+        finish_unit(*state["unit"], buf, state["uses"][buf])
+        state["uses"][buf] += 1
         state["buf"], state["unit"] = 1 - buf, (i, k)
 
     def run(i0, k0, width, start, count):
         buf = state["buf"]
+        uses = list(state["uses"])
 
         def unit(u):
             return i0 + u // width, k0 + u % width
 
         def body(it, carry):
             u = start + 2 * it
+            free(buf, uses[buf] + it)
+            free(1 - buf, uses[1 - buf] + it)
             dot(*unit(u), 1 - buf)
-            finish_unit(carry[0], carry[1], buf)
+            finish_unit(carry[0], carry[1], buf, uses[buf] + it)
             dot(*unit(u + 1), buf)
-            finish_unit(*unit(u), 1 - buf)
+            finish_unit(*unit(u), 1 - buf, uses[1 - buf] + it)
             return unit(u + 1)
 
         last = tuple(jnp.int32(v) for v in state["unit"])
         state["unit"] = lax.fori_loop(0, count // 2, body, last)
+        state["uses"] = [v + count // 2 for v in uses]
         if count % 2:
             one(*unit(jnp.int32(start + count - 1)))
 
@@ -239,9 +276,7 @@
     dot(0, 0, 0)
     img.wait(("p0", 1), ("m0", 0))
     got_cross(4, 3, 1)
-    one(0, 1, True)
-    one(0, 2, True)
-    run(0, 0, 4, 3, 13)
+    run(0, 0, 4, 1, 15)
     got_img(4, 3, 1)
     for r in (txt, img):
         r.wait(("f0", 0), ("f0", 1))
@@ -266,7 +301,7 @@
     got_cross(6)
     run(7, 0, 8, 0, 8)
     run(0, 7, 1, 0, 7)
-    finish_unit(*state["unit"], state["buf"])
+    last_unit()
 
     for p in range(16):
         for q in range(n // 128):
@@ -315,7 +350,8 @@
     part_ref[0:1, :] = (jnp.sum(loss, axis=0, keepdims=True) - diag) * inv
     part_ref[1:2, :] = (dt - diag) * inv
     for buf in (0, 1):
-        store(0, 0, buf).wait()
+        for slot in range(DEEP):
+            store(0, 0, buf, slot).wait()
     for copy in saves:
         copy.wait()
     net.finish()
@@ -334,11 +370,11 @@
         in_specs=[pl.BlockSpec(memory_space=pltpu.SMEM), vmem, vmem],
         out_specs=[hbm, hbm, hbm, vmem, vmem, vmem],
         scratch_shapes=[pltpu.VMEM((8, n, d), BF16), pltpu.VMEM((16, n, d), BF16), pltpu.VMEM((8, d, n), BF16),
-                        pltpu.VMEM((2, n, n), F32), pltpu.VMEM((2, n, n), F32), pltpu.VMEM((2, n, n), F32),
-                        pltpu.VMEM((2, n, n), F32), pltpu.VMEM((8 * n, 128), F32), pltpu.VMEM((8 * n, 128), F32),
+                        pltpu.VMEM((2, n, n), F32), pltpu.VMEM((2, n, n), F32), pltpu.VMEM((DEEP, 2, n, n), F32),
+                        pltpu.VMEM((DEEP, 2, n, n), F32), pltpu.VMEM((8 * n, 128), F32), pltpu.VMEM((8 * n, 128), F32),
                         pltpu.VMEM((16, 8, n), F32), pltpu.VMEM((16, 8, n), F32), pltpu.VMEM((16, 128), F32),
                         pltpu.VMEM((32, 128), F32), pltpu.VMEM((8, 16, 128), F32), pltpu.VMEM((16, 32, 128), F32),
-                        dma((2,)), dma((16,)), dma((8,)), dma((2,)), dma((N_FORWARD,)), dma((N_FORWARD,))],
+                        dma((2 * DEEP,)), dma((16,)), dma((8,)), dma((2,)), dma((N_FORWARD,)), dma((N_FORWARD,))],
         compiler_params=pltpu.CompilerParams(collective_id=0, has_side_effects=True, vmem_limit_bytes=VMEM_LIMIT),
         name="forward_sums")(scale, img, txt)
 
@@ -346,7 +382,6 @@
 ICUT = 144
 TCUT = 432
 ORDER = (6, 5, 7, 2, 1, 4, 3, 0)
-KC = 512
 N_REDUCE = 8 + 2 * (4 + 18 + 1) + 22
 
 
@@ -359,11 +394,11 @@
 
     def pair_send(self, d):
         at = pl.ds(self.cut, self.rows - self.cut)
-        self.early[d] = self.net.send(self.acc.at[4 + d, at], self.buf.at[4 + d, at], self.pair)
+        self.early[d] = self.net.send((self.acc, (POS[4 + d], at)), (self.buf, (4 + d, at)), self.pair)
 
     def pair_add(self, d):
         self.early[d].wait_recv()
-        self.acc[d, self.cut:] += self.buf[4 + d, self.cut:]
+        self.acc[POS[d], self.cut:] += self.buf[4 + d, self.cut:]
 
     def where(self, name):
         if name == 2:
@@ -373,7 +408,7 @@
     def send(self, name, key, slot, half, to_slot, peer):
         _, lo, h = self.where(name)
         at = pl.ds(lo + half * h, h)
-        self.streams[name, key] = self.net.send(self.acc.at[slot, at], self.buf.at[to_slot, at], peer)
+        self.streams[name, key] = self.net.send((self.acc, (POS[slot], at)), (self.buf, (to_slot, at)), peer)
 
     def far(self, name):
         b, _, _ = self.where(name)
@@ -391,21 +426,21 @@
     def mid(self, name):
         b, lo, h = self.where(name)
         self.streams[name, "a+"].wait_recv()
-        self.acc[b + 1, lo:lo + h] += self.buf[b + 2, lo:lo + h]
+        self.acc[POS[b + 1], lo:lo + h] += self.buf[b + 2, lo:lo + h]
         self.send(name, "b+0", b + 1, 0, b + 3, self.plus)
         self.streams[name, "a-"].wait_recv()
-        self.acc[b + 3, lo + h:lo + 2 * h] += self.buf[b + 2, lo + h:lo + 2 * h]
+        self.acc[POS[b + 3], lo + h:lo + 2 * h] += self.buf[b + 2, lo + h:lo + 2 * h]
         self.send(name, "b-1", b + 3, 1, b + 1, self.minus)
 
     def end(self, name):
         b, lo, h = self.where(name)
         for key in ("b+1", "b-0", "b+0", "b-1"):
             self.streams[name, key].wait_recv()
-        self.acc[b, lo:lo + 2 * h] += self.buf[b + 1, lo:lo + 2 * h] + self.buf[b + 3, lo:lo + 2 * h]
+        self.acc[POS[b], lo:lo + 2 * h] += self.buf[b + 1, lo:lo + 2 * h] + self.buf[b + 3, lo:lo + 2 * h]
 
     def pair_last(self):
         at = pl.ds(0, self.cut)
-        self.late = self.net.send(self.acc.at[4, at], self.buf.at[0, at], self.pair)
+        self.late = self.net.send((self.acc, (POS[4], at)), (self.buf, (0, at)), self.pair)
 
     def pair_end(self):
         self.late.wait_recv()
@@ -439,6 +474,7 @@
             self.pair_add(3)
             self.plain_minus(2)
             self.mid(0)
+            self.mid(2)
 
     def close(self):
         self.pair_add(0)
@@ -447,7 +483,10 @@
         self.end(2)
 
 
-def grads_kernel(inv, imgt_hbm, txt_hbm, e_hbm, a_ref, b_ref, part_ref, img_out, txt_out, part_out,
+KC = 512
+
+
+def grads_kernel(inv, scale_ref, imgt_hbm, txt_hbm, e_hbm, a_ref, b_ref, part_ref, img_out, txt_out, part_out,
                  imgt, txt, erow, ecol, gb0, gb1, arow, stage, iacc, tacc, ibuf, tbuf, dbuf, pa, pb, psum,
                  local_sems, row_sems, col_sems, send_sems, recv_sems):
     g = Grid()
@@ -492,6 +531,10 @@
         c = lax.broadcasted_iota(jnp.int32, (n, 128), 1) + q * 128
         return grad - jnp.where(r == c, 2.0 * inv, 0.0)
 
+    def add(out_ref, part, may_start, it):
+        old = out_ref[...]
+        out_ref[...] = part + (jnp.where(it > 0, old, 0.0) if may_start else old)
+
     def col_slot(p, e_ref, out_ref):
         b = [b_ref[2 * p + q:2 * p + q + 1, :] for q in range(n // 128)]
         tiles = KC // n
@@ -508,13 +551,11 @@
                     to[t * n:(t + 1) * n, lanes] = v.astype(BF16)
 
         grad(0, gb0[0], diag=p == 0)
-        out_ref[...] = jnp.zeros_like(out_ref)
-
         def body(it, carry):
             for half, (now, later) in enumerate(((gb0[0], gb0[1]), (gb0[1], gb0[0]))):
                 i = 2 * it + half
                 at = pl.ds(pl.multiple_of(i * KC, KC), KC)
-                out_ref[...] += jnp.dot(imgt[:, at], now[...], preferred_element_type=F32)
+                add(out_ref, jnp.dot(imgt[:, at], now[...], preferred_element_type=F32), half == 0, it)
                 grad((i + 1) % count, later)
             return carry
 
@@ -536,13 +577,11 @@
                     to[:, t * n + q * 128:t * n + (q + 1) * 128] = v.astype(BF16)
 
         grad(0, gb1[0], diag=p == 0)
-        out_ref[...] = jnp.zeros_like(out_ref)
-
         def body(it, carry):
             for half, (now, later) in enumerate(((gb1[0], gb1[1]), (gb1[1], gb1[0]))):
                 i = 2 * it + half
                 at = pl.ds(pl.multiple_of(i * KC, KC), KC)
-                out_ref[...] += jnp.dot(now[...], txt[at, :], preferred_element_type=F32)
+                add(out_ref, jnp.dot(now[...], txt[at, :], preferred_element_type=F32), half == 0, it)
                 grad((i + 1) % count, later)
             return carry
 
@@ -565,15 +604,15 @@
         rows[step].wait()
         if step == 0:
             load_txt.wait()
-        row_slot(POS[k], erow.at[step % 2], iacc.at[k])
+        row_slot(POS[k], erow.at[step % 2], iacc.at[POS[k]])
         img.ready(step)
         cols[step, 0].wait()
-        col_slot(POS[k], ecol.at[0], tacc.at[k])
+        col_slot(POS[k], ecol.at[0], tacc.at[POS[k]])
         if step + 1 < len(ORDER):
             cols[step + 1, 0] = col_load(step + 1, 0)
             cols[step + 1, 0].start()
         cross[k].wait_recv()
-        tacc[k] += dbuf[k]
+        tacc[POS[k]] += dbuf[k]
         txr.ready(step)
         if step == 1:
             for copy in scal_a:
@@ -584,8 +623,6 @@
             psum[...] = total
             scal_b = [net.send(psum, pb.at[ib], g.txt_peer(*o)) for o in txt_offs]
             pb[ib] = total
-    for r in (img, txr):
-        r.mid(2)
     for copy in scal_b:
         copy.wait_recv()
     total = pb[0]
@@ -594,12 +631,13 @@
     part_out[...] = total
     for r in (img, txr):
         r.close()
-    img_out[...] = iacc[0]
-    txt_out[...] = tacc[0]
+    scale = scale_ref[0]
+    img_out[...] = (scale * iacc[0]).astype(BF16)
+    txt_out[...] = (scale * tacc[0]).T.astype(BF16)
     net.finish(skip=[cross[k] for k in ORDER[:-2]])
 
 
-def grads(inv, imgt, txt_all, e, a, b, part):
+def grads(inv, scale, imgt, txt_all, e, a, b, part):
     d, m = imgt.shape
     nt = txt_all.shape[0]
     n = m // 8
@@ -608,9 +646,9 @@
     dma = pltpu.SemaphoreType.DMA
     return pl.pallas_call(
         functools.partial(grads_kernel, inv),
-        out_shape=[jax.ShapeDtypeStruct((n, d), F32), jax.ShapeDtypeStruct((d, n), F32),
+        out_shape=[jax.ShapeDtypeStruct((n, d), BF16), jax.ShapeDtypeStruct((n, d), BF16),
                    jax.ShapeDtypeStruct((8, 128), F32)],
-        in_specs=[hbm, hbm, hbm, vmem, vmem, vmem],
+        in_specs=[pl.BlockSpec(memory_space=pltpu.SMEM), hbm, hbm, hbm, vmem, vmem, vmem],
         out_specs=[vmem] * 3,
         scratch_shapes=[pltpu.VMEM((d, m), BF16), pltpu.VMEM((nt, d), BF16), pltpu.VMEM((2, 2, 8, n, n), F32),
                         pltpu.VMEM((2, 8, n, n), F32), [pltpu.VMEM((KC, n), BF16)] * 2, [pltpu.VMEM((n, KC), BF16)] * 2,
@@ -621,7 +659,7 @@
                         dma((N_REDUCE,))],
         compiler_params=pltpu.CompilerParams(collective_id=2, has_side_effects=True, vmem_limit_bytes=VMEM_LIMIT),
         cost_estimate=pl.CostEstimate(flops=4 * m * nt * d, bytes_accessed=8 * m * nt, transcendentals=0),
-        name="grads_reduce")(imgt, txt_all, e, a, b, part)
+        name="grads_reduce")(scale, imgt, txt_all, e, a, b, part)
 
 
 def solution(mesh):
@@ -633,9 +671,7 @@
         inv = 1.0 / (2 * n * shards)
         scale = jnp.exp(log_scale)
         e, imgt, txt_all, a, b, part = forward(inv, scale.reshape(1), img_loc, txt_loc)
-        img_sum, txt_sum, tot = grads(inv, imgt, txt_all, e, a, b, part)
-        d_img = (scale * img_sum).astype(BF16)
-        d_txt = (scale * txt_sum).T.astype(BF16)
+        d_img, d_txt, tot = grads(inv, scale.reshape(1), imgt, txt_all, e, a, b, part)
         tot = jnp.sum(tot[0:2], axis=1)
         return tot[0], d_img, d_txt, tot[1]
 

time: 140 us -> 125 us (0.89)
  Pallas kernels: 133 us -> 119 us
  other arithmetic: 3.9 us -> 0.8 us
  local copies, waits for them, and re-layouts: 1.51 us -> 4.12 us
    pallas_call x1, Pallas kernels: 69.3 us -> 55.4 us  [forward(): pl.pallas_call(functools.partial(forward_kernel, inv), out_shape=[jax.Sha...]
    convert_element_type x2 -> x0, other arithmetic: 3.12 us -> none  [the longest x1 1.92 us: local_tile(): d_img = (scale * img_sum).astype(BF16)]
    unnamed x1 -> x2, local copies, waits for them, and re-layouts: 0.92 us -> 3.53 us
where the time goes in v5:
time: 125 us
  Pallas kernels  119 us (95%)
  local copies, waits for them, and re-layouts  4.12 us (3%)
  between operations  1.34 us (1%)
    pallas_call x1, Pallas kernels, grads(): pl.pallas_call(functools.partial(grads_kernel, inv), out_shape=[jax.Shape...  63.4 us
    pallas_call x1, Pallas kernels, forward(): pl.pallas_call(functools.partial(forward_kernel, inv), out_shape=[jax.Sha...  55.4 us
    unnamed x2, local copies, waits for them, and re-layouts  3.53 us

profile of v5, /device:TPU:1, one launch (start us, length us, event | category | flops | bytes accessed | tf_op | source)
XLA Modules:
  0.0 125.1 jit_solution(16869184432492778718)
XLA Ops:
  1.3 55.4 %forward_sums.1 = (f32[8,2,8,256,256]{4,3,2,1,0:T(8,128)}, bf16[768,2048]{1,0:T(8,128)(2,1)}, bf16[4096,768]{1,0:T(8,128)(2,1)}, f32[16,128]{1,0:T(8,128)}, f32[32,128]{1,0:T(8,128)}, /*index=5*/f32[8,128]{1,0:T(8,128)}) custom-call(f32[1]{0:T(128)} %bitcast.scale_ref, bf16[256,768]{1,0:T(8,128)(2,1)} %img_ref.1, bf16[256,768]{1,0:T(8,128)(2,1)} %txt_ref.1), custom_call_target="tpu_custom_call" | custom-call | tf_op jit(solution)/shard_map/forward_sums/pallas_call | solution.py:365
  56.8 63.4 %grads_reduce.1 = (bf16[256,768]{1,0:T(8,128)(2,1)}, bf16[256,768]{1,0:T(8,128)(2,1)}, f32[8,128]{1,0:T(8,128)}) custom-call(f32[1]{0:T(128)} %bitcast.scale_ref, bf16[768,2048]{1,0:T(8,128)(2,1)} %get-tuple-element.13.imgt_hbm, bf16[4096,768]{1,0:T(8,128)(2,1)} %get-tuple-element.14.txt_hbm, f32[8,2,8,256,256]{4,3,2,1,0:T(8,128)} %get-tuple-element.15.e_hbm, ...), custom_call_target="tpu_custom_call" | custom-call | flops 25769803776 | bytes 67108864 | tf_op jit(solution)/shard_map/grads_reduce/pallas_call | solution.py:647
  120.1 0.8 slice_reduce_fusion
  120.9 0.6 fusion
  121.5 1.8 %copy.10 = bf16[256,768]{1,0:T(8,128)(2,1)} copy(bf16[256,768]{1,0:T(8,128)(2,1)} %get-tuple-element.29) | data formatting | bytes 786432
  123.3 1.8 %copy.11 = bf16[256,768]{1,0:T(8,128)(2,1)} copy(bf16[256,768]{1,0:T(8,128)(2,1)} %get-tuple-element.30) | data formatting | bytes 786432

commit v6 on v5

--- a/solution.py
+++ b/solution.py
@@ -486,7 +486,7 @@
 KC = 512
 
 
-def grads_kernel(inv, scale_ref, imgt_hbm, txt_hbm, e_hbm, a_ref, b_ref, part_ref, img_out, txt_out, part_out,
+def grads_kernel(inv, imgt_hbm, txt_hbm, e_hbm, a_ref, b_ref, part_ref, img_out, txt_out, part_out,
                  imgt, txt, erow, ecol, gb0, gb1, arow, stage, iacc, tacc, ibuf, tbuf, dbuf, pa, pb, psum,
                  local_sems, row_sems, col_sems, send_sems, recv_sems):
     g = Grid()
@@ -506,14 +506,13 @@
     load_imgt = pltpu.make_async_copy(imgt_hbm, imgt, local_sems.at[0])
     load_txt = pltpu.make_async_copy(txt_hbm, txt, local_sems.at[1])
     cols = {}
-    cols[0, 1] = col_load(0, 1)
-    cols[0, 1].start()
+    for side in (1, 0):
+        cols[0, side] = col_load(0, side)
+        cols[0, side].start()
     load_imgt.start()
     rows = {0: row_load(0)}
     rows[0].start()
     load_txt.start()
-    cols[0, 0] = col_load(0, 0)
-    cols[0, 0].start()
     for i in range(m // 128):
         arow[i * 128:(i + 1) * 128, :] = jnp.broadcast_to(a_ref[i:i + 1, :], (128, 128)).T
     greet([g.img_peer(*o) for o in img_offs] + [g.txt_peer(*o) for o in txt_offs])
@@ -535,27 +534,31 @@
         old = out_ref[...]
         out_ref[...] = part + (jnp.where(it > 0, old, 0.0) if may_start else old)
 
-    def col_slot(p, e_ref, out_ref):
-        b = [b_ref[2 * p + q:2 * p + q + 1, :] for q in range(n // 128)]
+    def col_slots(p, outs):
         tiles = KC // n
         count = m // KC
 
         def grad(i, to, diag=False):
             for t in range(tiles):
-                for q in range(n // 128):
-                    lanes = slice(q * 128, (q + 1) * 128)
-                    a = arow[pl.ds(pl.multiple_of(i * KC + t * n, n), n), :]
-                    v = e_ref[i * tiles + t, :, lanes] * (a + b[q])
-                    if diag and t == 0:
-                        v = minus_diag(v, q)
-                    to[t * n:(t + 1) * n, lanes] = v.astype(BF16)
+                a = arow[pl.ds(pl.multiple_of(i * KC + t * n, n), n), :]
+                for side in (0, 1):
+                    for q in range(n // 128):
+                        lanes = slice(q * 128, (q + 1) * 128)
+                        at = 2 * (p + 8 * side) + q
+                        v = ecol[side, i * tiles + t, :, lanes] * (a + b_ref[at:at + 1, :])
+                        if diag and t == 0 and side == 0:
+                            v = minus_diag(v, q)
+                        to[t * n:(t + 1) * n, side * n + q * 128:side * n + (q + 1) * 128] = v.astype(BF16)
 
         grad(0, gb0[0], diag=p == 0)
+
         def body(it, carry):
             for half, (now, later) in enumerate(((gb0[0], gb0[1]), (gb0[1], gb0[0]))):
                 i = 2 * it + half
                 at = pl.ds(pl.multiple_of(i * KC, KC), KC)
-                add(out_ref, jnp.dot(imgt[:, at], now[...], preferred_element_type=F32), half == 0, it)
+                part = jnp.dot(imgt[:, at], now[...], preferred_element_type=F32)
+                for side in (0, 1):
+                    add(outs[side], part[:, side * n:(side + 1) * n], half == 0, it)
                 grad((i + 1) % count, later)
             return carry
 
@@ -590,30 +593,27 @@
     cross = {}
     for step, k in enumerate(ORDER):
         cols[step, 1].wait()
+        cols[step, 0].wait()
         if step == 0:
             load_imgt.wait()
         if step >= 2:
             cross[ORDER[step - 2]].wait_send()
-        col_slot(8 + POS[k], ecol.at[1], stage.at[step % 2])
+        col_slots(POS[k], (tacc.at[POS[k]], stage.at[step % 2]))
         cross[k] = net.send(stage.at[step % 2], dbuf.at[k], core)
         if step + 1 < len(ORDER):
-            cols[step + 1, 1] = col_load(step + 1, 1)
-            cols[step + 1, 1].start()
             rows[step + 1] = row_load(step + 1)
             rows[step + 1].start()
+            for side in (1, 0):
+                cols[step + 1, side] = col_load(step + 1, side)
+                cols[step + 1, side].start()
         rows[step].wait()
         if step == 0:
             load_txt.wait()
         row_slot(POS[k], erow.at[step % 2], iacc.at[POS[k]])
-        img.ready(step)
-        cols[step, 0].wait()
-        col_slot(POS[k], ecol.at[0], tacc.at[POS[k]])
-        if step + 1 < len(ORDER):
-            cols[step + 1, 0] = col_load(step + 1, 0)
-            cols[step + 1, 0].start()
         cross[k].wait_recv()
         tacc[POS[k]] += dbuf[k]
         txr.ready(step)
+        img.ready(step)
         if step == 1:
             for copy in scal_a:
                 copy.wait_recv()
@@ -631,13 +631,12 @@
     part_out[...] = total
     for r in (img, txr):
         r.close()
-    scale = scale_ref[0]
-    img_out[...] = (scale * iacc[0]).astype(BF16)
-    txt_out[...] = (scale * tacc[0]).T.astype(BF16)
+    img_out[...] = iacc[0]
+    txt_out[...] = tacc[0].T
     net.finish(skip=[cross[k] for k in ORDER[:-2]])
 
 
-def grads(inv, scale, imgt, txt_all, e, a, b, part):
+def grads(inv, imgt, txt_all, e, a, b, part):
     d, m = imgt.shape
     nt = txt_all.shape[0]
     n = m // 8
@@ -646,12 +645,12 @@
     dma = pltpu.SemaphoreType.DMA
     return pl.pallas_call(
         functools.partial(grads_kernel, inv),
-        out_shape=[jax.ShapeDtypeStruct((n, d), BF16), jax.ShapeDtypeStruct((n, d), BF16),
+        out_shape=[jax.ShapeDtypeStruct((n, d), F32), jax.ShapeDtypeStruct((n, d), F32),
                    jax.ShapeDtypeStruct((8, 128), F32)],
-        in_specs=[pl.BlockSpec(memory_space=pltpu.SMEM), hbm, hbm, hbm, vmem, vmem, vmem],
+        in_specs=[hbm, hbm, hbm, vmem, vmem, vmem],
         out_specs=[vmem] * 3,
         scratch_shapes=[pltpu.VMEM((d, m), BF16), pltpu.VMEM((nt, d), BF16), pltpu.VMEM((2, 2, 8, n, n), F32),
-                        pltpu.VMEM((2, 8, n, n), F32), [pltpu.VMEM((KC, n), BF16)] * 2, [pltpu.VMEM((n, KC), BF16)] * 2,
+                        pltpu.VMEM((2, 8, n, n), F32), [pltpu.VMEM((KC, 2 * n), BF16)] * 2, [pltpu.VMEM((n, KC), BF16)] * 2,
                         pltpu.VMEM((m, 128), F32), pltpu.VMEM((2, d, n), F32), pltpu.VMEM((8, n, d), F32),
                         pltpu.VMEM((8, d, n), F32), pltpu.VMEM((8, n, d), F32), pltpu.VMEM((8, d, n), F32),
                         pltpu.VMEM((8, d, n), F32), pltpu.VMEM((8, 8, 128), F32), pltpu.VMEM((16, 8, 128), F32),
@@ -659,7 +658,7 @@
                         dma((N_REDUCE,))],
         compiler_params=pltpu.CompilerParams(collective_id=2, has_side_effects=True, vmem_limit_bytes=VMEM_LIMIT),
         cost_estimate=pl.CostEstimate(flops=4 * m * nt * d, bytes_accessed=8 * m * nt, transcendentals=0),
-        name="grads_reduce")(scale, imgt, txt_all, e, a, b, part)
+        name="grads_reduce")(imgt, txt_all, e, a, b, part)
 
 
 def solution(mesh):
@@ -671,7 +670,9 @@
         inv = 1.0 / (2 * n * shards)
         scale = jnp.exp(log_scale)
         e, imgt, txt_all, a, b, part = forward(inv, scale.reshape(1), img_loc, txt_loc)
-        d_img, d_txt, tot = grads(inv, scale.reshape(1), imgt, txt_all, e, a, b, part)
+        img_sum, txt_sum, tot = grads(inv, imgt, txt_all, e, a, b, part)
+        d_img = (scale * img_sum).astype(BF16)
+        d_txt = (scale * txt_sum).astype(BF16)
         tot = jnp.sum(tot[0:2], axis=1)
         return tot[0], d_img, d_txt, tot[1]
 

time: 125 us -> 126 us (level)
  local copies, waits for them, and re-layouts: 4.12 us -> 0.59 us
  other arithmetic: 0.8 us -> 3.15 us
  Pallas kernels: 119 us -> 121 us
    unnamed x2 -> x0, local copies, waits for them, and re-layouts: 3.53 us -> none
    convert_element_type x0 -> x1, other arithmetic: none -> 2.35 us  [local_tile(): d_txt = (scale * txt_sum).astype(BF16)]
    pallas_call x1, Pallas kernels: 63.4 us -> 65.6 us  [grads(): pl.pallas_call(functools.partial(grads_kernel, inv), out_shape=[jax.Shape...]
where the time goes in v6:
time: 126 us
  Pallas kernels  121 us (96%)
  other arithmetic  3.15 us (2%)
  between operations  1.34 us (1%)
    pallas_call x1, Pallas kernels, grads(): pl.pallas_call(functools.partial(grads_kernel, inv), out_shape=[jax.Shape...  65.6 us
    pallas_call x1, Pallas kernels, forward(): pl.pallas_call(functools.partial(forward_kernel, inv), out_shape=[jax.Sha...  55.4 us

profile of v6, /device:TPU:1, one launch (start us, length us, event | category | flops | bytes accessed | tf_op | source)
XLA Modules:
  0.0 126.1 jit_solution(4606816776328013726)
XLA Ops:
  1.3 55.4 %forward_sums.1 = (f32[8,2,8,256,256]{4,3,2,1,0:T(8,128)}, bf16[768,2048]{1,0:T(8,128)(2,1)}, bf16[4096,768]{1,0:T(8,128)(2,1)}, f32[16,128]{1,0:T(8,128)}, f32[32,128]{1,0:T(8,128)}, /*index=5*/f32[8,128]{1,0:T(8,128)}) custom-call(f32[1]{0:T(128)} %bitcast.scale_ref, bf16[256,768]{1,0:T(8,128)(2,1)} %img_ref.1, bf16[256,768]{1,0:T(8,128)(2,1)} %txt_ref.1), custom_call_target="tpu_custom_call" | custom-call | tf_op jit(solution)/shard_map/forward_sums/pallas_call | solution.py:365
  56.7 65.6 %grads_reduce.1 = (f32[256,768]{1,0:T(8,128)}, f32[256,768]{1,0:T(8,128)}, f32[8,128]{1,0:T(8,128)}) custom-call(bf16[768,2048]{1,0:T(8,128)(2,1)} %get-tuple-element.13.imgt_hbm, bf16[4096,768]{1,0:T(8,128)(2,1)} %get-tuple-element.14.txt_hbm, f32[8,2,8,256,256]{4,3,2,1,0:T(8,128)} %get-tuple-element.15.e_hbm, f32[16,128]{1,0:T(8,128)} %get-tuple-element.16.a_ref, ...), custom_call_target="tpu_custom_call" | custom-call | flops 25769803776 | bytes 67108864 | tf_op jit(solution)/shard_map/grads_reduce/pallas_call | solution.py:646
  122.4 0.8 slice_reduce_fusion
  123.2 0.6 fusion
  123.7 2.4 %multiply_convert_fusion = (bf16[256,768]{1,0:T(8,128)(2,1)}, bf16[256,768]{1,0:T(8,128)(2,1)}) fusion(f32[256,768]{1,0:T(8,128)} %get-tuple-element.21, f32[]{:T(128)} %exp.3, f32[256,768]{1,0:T(8,128)} %get-tuple-element.20), kind=kLoop, calls=%fused_computation | loop fusion | flops 786432 | bytes 2359300 | tf_op jit(solution)/shard_map/convert_element_type | solution.py:675

commit v7 on v5

--- a/solution.py
+++ b/solution.py
@@ -20,6 +20,7 @@
         self.z = row // 16
         self.y = (row // 4) % 4
         self.x = row % 4
+        self.turn = 1 - 2 * self.c
 
     def dev(self, z, y, x, c):
         return {"row": (z * 4 + y) * 4 + x, "col": c}
@@ -32,12 +33,12 @@
 
     def img_peer(self, dy, dz):
         y = self.y_a() if dy else self.y
-        return self.dev((self.z + dz) % 4, y, self.x, self.c)
+        return self.dev((self.z + 4 + self.turn * dz) % 4, y, self.x, self.c)
 
     def txt_peer(self, dc, dy, dx):
         y = self.y_b() if dy else self.y
         c = 1 - self.c if dc else self.c
-        return self.dev(self.z, y, (self.x + dx) % 4, c)
+        return self.dev(self.z, y, (self.x + 4 + self.turn * dx) % 4, c)
 
 
 def view(ref):
@@ -91,6 +92,10 @@
 POS = {0: 0, 3: 1, 4: 2, 1: 3, 2: 4, 7: 5, 5: 6, 6: 7}
 DEEP = 4
 N_FORWARD = 2 * 18 + 9 + 22
+
+
+def mirror(k):
+    return 4 * (k // 4) + (4 - k % 4) % 4
 
 
 class Gather:
@@ -162,12 +167,12 @@
     def got_txt(*slots):
         for k in slots:
             p = POS[k]
-            cross[p] = net.send(txt_all.at[p], txt_all.at[8 + p], core)
+            cross[k] = net.send(txt_all.at[p], txt_all.at[8 + POS[mirror(k)]], core)
             save_txt(p)
 
     def got_cross(*slots):
         for k in slots:
-            cross[POS[k]].wait_recv()
+            cross[mirror(k)].wait_recv()
             save_txt(8 + POS[k])
 
     def got_img(*slots):
@@ -308,7 +313,7 @@
             csum[2 * p + q:2 * p + q + 1, :] = jnp.sum(cs[p, :, q * 128:(q + 1) * 128], axis=0, keepdims=True)
     sums = []
     for dc, dy, dx in txt_offs:
-        sums.append(net.send(csum, cbuf.at[dc * 8 + dy * 4 + (4 - dx) % 4], g.txt_peer(dc, dy, dx)))
+        sums.append(net.send(csum, cbuf.at[dc * 8 + dy * 4 + (dx if dc else (4 - dx) % 4)], g.txt_peer(dc, dy, dx)))
     for i in range(8 * n // 128):
         rsum[i:i + 1, :] = jnp.sum(rs[i * 128:(i + 1) * 128, :].T, axis=0, keepdims=True)
     for dy, dz in img_offs:
@@ -336,7 +341,7 @@
         k = 2 * (dc * 8 + POS[dy * 4 + dx])
         tot = csum[k:k + 2, :]
         for oc, oy, ox in txt_offs:
-            q = 2 * ((dc ^ oc) * 8 + POS[(dy ^ oy) * 4 + (dx - ox) % 4])
+            q = 2 * ((dc ^ oc) * 8 + POS[(dy ^ oy) * 4 + ((ox - dx) if oc else (dx - ox)) % 4])
             tot += cbuf[oc * 8 + oy * 4 + ox, q:q + 2, :]
         b = 1.0 / tot
         b_ref[k:k + 2, :] = b * inv
@@ -486,7 +491,7 @@
 KC = 512
 
 
-def grads_kernel(inv, scale_ref, imgt_hbm, txt_hbm, e_hbm, a_ref, b_ref, part_ref, img_out, txt_out, part_out,
+def grads_kernel(inv, imgt_hbm, txt_hbm, e_hbm, a_ref, b_ref, part_ref, img_out, txt_out, part_out,
                  imgt, txt, erow, ecol, gb0, gb1, arow, stage, iacc, tacc, ibuf, tbuf, dbuf, pa, pb, psum,
                  local_sems, row_sems, col_sems, send_sems, recv_sems):
     g = Grid()
@@ -501,7 +506,8 @@
         return pltpu.make_async_copy(e_hbm.at[POS[ORDER[step]]], erow.at[step % 2], row_sems.at[step % 2])
 
     def col_load(step, side):
-        return pltpu.make_async_copy(e_hbm.at[:, side, POS[ORDER[step]]], ecol.at[side], col_sems.at[side])
+        k = mirror(ORDER[step]) if side else ORDER[step]
+        return pltpu.make_async_copy(e_hbm.at[:, side, POS[k]], ecol.at[side], col_sems.at[side])
 
     load_imgt = pltpu.make_async_copy(imgt_hbm, imgt, local_sems.at[0])
     load_txt = pltpu.make_async_copy(txt_hbm, txt, local_sems.at[1])
@@ -594,7 +600,7 @@
             load_imgt.wait()
         if step >= 2:
             cross[ORDER[step - 2]].wait_send()
-        col_slot(8 + POS[k], ecol.at[1], stage.at[step % 2])
+        col_slot(8 + POS[mirror(k)], ecol.at[1], stage.at[step % 2])
         cross[k] = net.send(stage.at[step % 2], dbuf.at[k], core)
         if step + 1 < len(ORDER):
             cols[step + 1, 1] = col_load(step + 1, 1)
@@ -631,13 +637,12 @@
     part_out[...] = total
     for r in (img, txr):
         r.close()
-    scale = scale_ref[0]
-    img_out[...] = (scale * iacc[0]).astype(BF16)
-    txt_out[...] = (scale * tacc[0]).T.astype(BF16)
+    img_out[...] = iacc[0]
+    txt_out[...] = tacc[0].T
     net.finish(skip=[cross[k] for k in ORDER[:-2]])
 
 
-def grads(inv, scale, imgt, txt_all, e, a, b, part):
+def grads(inv, imgt, txt_all, e, a, b, part):
     d, m = imgt.shape
     nt = txt_all.shape[0]
     n = m // 8
@@ -646,9 +651,9 @@
     dma = pltpu.SemaphoreType.DMA
     return pl.pallas_call(
         functools.partial(grads_kernel, inv),
-        out_shape=[jax.ShapeDtypeStruct((n, d), BF16), jax.ShapeDtypeStruct((n, d), BF16),
+        out_shape=[jax.ShapeDtypeStruct((n, d), F32), jax.ShapeDtypeStruct((n, d), F32),
                    jax.ShapeDtypeStruct((8, 128), F32)],
-        in_specs=[pl.BlockSpec(memory_space=pltpu.SMEM), hbm, hbm, hbm, vmem, vmem, vmem],
+        in_specs=[hbm, hbm, hbm, vmem, vmem, vmem],
         out_specs=[vmem] * 3,
         scratch_shapes=[pltpu.VMEM((d, m), BF16), pltpu.VMEM((nt, d), BF16), pltpu.VMEM((2, 2, 8, n, n), F32),
                         pltpu.VMEM((2, 8, n, n), F32), [pltpu.VMEM((KC, n), BF16)] * 2, [pltpu.VMEM((n, KC), BF16)] * 2,
@@ -659,7 +664,7 @@
                         dma((N_REDUCE,))],
         compiler_params=pltpu.CompilerParams(collective_id=2, has_side_effects=True, vmem_limit_bytes=VMEM_LIMIT),
         cost_estimate=pl.CostEstimate(flops=4 * m * nt * d, bytes_accessed=8 * m * nt, transcendentals=0),
-        name="grads_reduce")(scale, imgt, txt_all, e, a, b, part)
+        name="grads_reduce")(imgt, txt_all, e, a, b, part)
 
 
 def solution(mesh):
@@ -671,7 +676,9 @@
         inv = 1.0 / (2 * n * shards)
         scale = jnp.exp(log_scale)
         e, imgt, txt_all, a, b, part = forward(inv, scale.reshape(1), img_loc, txt_loc)
-        d_img, d_txt, tot = grads(inv, scale.reshape(1), imgt, txt_all, e, a, b, part)
+        img_sum, txt_sum, tot = grads(inv, imgt, txt_all, e, a, b, part)
+        d_img = (scale * img_sum).astype(BF16)
+        d_txt = (scale * txt_sum).astype(BF16)
         tot = jnp.sum(tot[0:2], axis=1)
         return tot[0], d_img, d_txt, tot[1]
 

time: 125 us -> 122 us (0.976)
  local copies, waits for them, and re-layouts: 4.12 us -> 0.59 us
  Pallas kernels: 119 us -> 116 us
  other arithmetic: 0.8 us -> 3.15 us
    unnamed x2 -> x0, local copies, waits for them, and re-layouts: 3.53 us -> none
    pallas_call x1, Pallas kernels: 63.4 us -> 61 us  [grads(): pl.pallas_call(functools.partial(grads_kernel, inv), out_shape=[jax.Shape...]
    convert_element_type x0 -> x1, other arithmetic: none -> 2.35 us  [local_tile(): d_txt = (scale * txt_sum).astype(BF16)]
where the time goes in v7:
time: 122 us; the launch traced here: 121 us
  Pallas kernels  116 us (95%)
  other arithmetic  3.15 us (3%)
  between operations  1.34 us (1%)
    pallas_call x1, Pallas kernels, grads(): pl.pallas_call(functools.partial(grads_kernel, inv), out_shape=[jax.Shape...  61 us
    pallas_call x1, Pallas kernels, forward(): pl.pallas_call(functools.partial(forward_kernel, inv), out_shape=[jax.Sha...  55.3 us

profile of v7, /device:TPU:1, one launch (start us, length us, event | category | flops | bytes accessed | tf_op | source)
XLA Modules:
  0.0 121.4 jit_solution(9623255804579336974)
XLA Ops:
  1.3 55.3 %forward_sums.1 = (f32[8,2,8,256,256]{4,3,2,1,0:T(8,128)}, bf16[768,2048]{1,0:T(8,128)(2,1)}, bf16[4096,768]{1,0:T(8,128)(2,1)}, f32[16,128]{1,0:T(8,128)}, f32[32,128]{1,0:T(8,128)}, /*index=5*/f32[8,128]{1,0:T(8,128)}) custom-call(f32[1]{0:T(128)} %bitcast.scale_ref, bf16[256,768]{1,0:T(8,128)(2,1)} %img_ref.1, bf16[256,768]{1,0:T(8,128)(2,1)} %txt_ref.1), custom_call_target="tpu_custom_call" | custom-call | tf_op jit(solution)/shard_map/forward_sums/pallas_call | solution.py:370
  56.7 61.0 %grads_reduce.1 = (f32[256,768]{1,0:T(8,128)}, f32[256,768]{1,0:T(8,128)}, f32[8,128]{1,0:T(8,128)}) custom-call(bf16[768,2048]{1,0:T(8,128)(2,1)} %get-tuple-element.13.imgt_hbm, bf16[4096,768]{1,0:T(8,128)(2,1)} %get-tuple-element.14.txt_hbm, f32[8,2,8,256,256]{4,3,2,1,0:T(8,128)} %get-tuple-element.15.e_hbm, f32[16,128]{1,0:T(8,128)} %get-tuple-element.16.a_ref, ...), custom_call_target="tpu_custom_call" | custom-call | flops 25769803776 | bytes 67108864 | tf_op jit(solution)/shard_map/grads_reduce/pallas_call | solution.py:652
  117.7 0.8 slice_reduce_fusion
  118.5 0.6 fusion
  119.0 2.4 %multiply_convert_fusion = (bf16[256,768]{1,0:T(8,128)(2,1)}, bf16[256,768]{1,0:T(8,128)(2,1)}) fusion(f32[256,768]{1,0:T(8,128)} %get-tuple-element.21, f32[]{:T(128)} %exp.3, f32[256,768]{1,0:T(8,128)} %get-tuple-element.20), kind=kLoop, calls=%fused_computation | loop fusion | flops 786432 | bytes 2359300 | tf_op jit(solution)/shard_map/convert_element_type | solution.py:681

commit v8 on v7

--- a/solution.py
+++ b/solution.py
@@ -386,7 +386,7 @@
 
 ICUT = 144
 TCUT = 432
-ORDER = (6, 5, 7, 2, 1, 4, 3, 0)
+ORDER = (6, 5, 7, 4, 2, 1, 3, 0)
 N_REDUCE = 8 + 2 * (4 + 18 + 1) + 22
 
 
@@ -463,17 +463,17 @@
             self.plain_minus(1)
             self.mid(1)
         elif step == 3:
+            self.pair_send(0)
+        elif step == 4:
             self.far(0)
             self.pair_add(2)
             self.far(2)
-        elif step == 4:
+            self.end(1)
+            self.pair_last()
+        elif step == 5:
             self.plain_plus(0)
             self.pair_add(1)
             self.plain_plus(2)
-        elif step == 5:
-            self.pair_send(0)
-            self.end(1)
-            self.pair_last()
         elif step == 6:
             self.plain_minus(0)
             self.pair_add(3)

time: 122 us -> 123 us (level)
  Pallas kernels: 116 us -> 118 us
    pallas_call x1, Pallas kernels: 61 us -> 62.8 us  [grads(): pl.pallas_call(functools.partial(grads_kernel, inv), out_shape=[jax.Shape...]
where the time goes in v8:
time: 123 us
  Pallas kernels  118 us (96%)
  other arithmetic  3.15 us (3%)
  between operations  1.34 us (1%)
    pallas_call x1, Pallas kernels, grads(): pl.pallas_call(functools.partial(grads_kernel, inv), out_shape=[jax.Shape...  62.8 us
    pallas_call x1, Pallas kernels, forward(): pl.pallas_call(functools.partial(forward_kernel, inv), out_shape=[jax.Sha...  55.3 us

profile of v8, /device:TPU:1, one launch (start us, length us, event | category | flops | bytes accessed | tf_op | source)
XLA Modules:
  0.0 123.2 jit_solution(5956048642604501472)
XLA Ops:
  1.3 55.3 %forward_sums.1 = (f32[8,2,8,256,256]{4,3,2,1,0:T(8,128)}, bf16[768,2048]{1,0:T(8,128)(2,1)}, bf16[4096,768]{1,0:T(8,128)(2,1)}, f32[16,128]{1,0:T(8,128)}, f32[32,128]{1,0:T(8,128)}, /*index=5*/f32[8,128]{1,0:T(8,128)}) custom-call(f32[1]{0:T(128)} %bitcast.scale_ref, bf16[256,768]{1,0:T(8,128)(2,1)} %img_ref.1, bf16[256,768]{1,0:T(8,128)(2,1)} %txt_ref.1), custom_call_target="tpu_custom_call" | custom-call | tf_op jit(solution)/shard_map/forward_sums/pallas_call | solution.py:370
  56.7 62.8 %grads_reduce.1 = (f32[256,768]{1,0:T(8,128)}, f32[256,768]{1,0:T(8,128)}, f32[8,128]{1,0:T(8,128)}) custom-call(bf16[768,2048]{1,0:T(8,128)(2,1)} %get-tuple-element.13.imgt_hbm, bf16[4096,768]{1,0:T(8,128)(2,1)} %get-tuple-element.14.txt_hbm, f32[8,2,8,256,256]{4,3,2,1,0:T(8,128)} %get-tuple-element.15.e_hbm, f32[16,128]{1,0:T(8,128)} %get-tuple-element.16.a_ref, ...), custom_call_target="tpu_custom_call" | custom-call | flops 25769803776 | bytes 67108864 | tf_op jit(solution)/shard_map/grads_reduce/pallas_call | solution.py:652
  119.5 0.8 slice_reduce_fusion
  120.3 0.6 fusion
  120.8 2.4 %multiply_convert_fusion = (bf16[256,768]{1,0:T(8,128)(2,1)}, bf16[256,768]{1,0:T(8,128)(2,1)}) fusion(f32[256,768]{1,0:T(8,128)} %get-tuple-element.21, f32[]{:T(128)} %exp.3, f32[256,768]{1,0:T(8,128)} %get-tuple-element.20), kind=kLoop, calls=%fused_computation | loop fusion | flops 786432 | bytes 2359300 | tf_op jit(solution)/shard_map/convert_element_type | solution.py:681
